TPU v7x, 32 devices: a whole 2x2x4 slice. The times are simulated.
32 devices in a mesh: grp: 4 (over z), seq: 8 (over y, x, core).
Axes of the slice: x: 2, y: 2, z: 4, core: 2. Of those that a mesh axis runs over, the one named last changes fastest.
Arguments:
- latent: bfloat16 [4, 256, 32, 256], P('grp', 'seq'), may hold values from -6 to 6
- up_key: bfloat16 [4, 128, 256], replicated, may hold values from -0.5 to 0.5
- up_value: bfloat16 [4, 128, 256], replicated, may hold values from -0.5 to 0.5
- queries: bfloat16 [8, 64, 128], replicated, may hold values from -240 to 240, as said below
- lengths: int32 [8], replicated, may hold values from 1 to 1024
- block_dest: int32 [256], replicated, may hold values from 0 to 31, as said below
Outputs:
- decode_latent: bfloat16 [32, 4, 8, 32, 256], P(('grp', 'seq'))
- attended: float32 [8, 8192], replicated
Inputs may be any that keep to these rules, and one draw needn't show every extreme that they name: `block_dest`: each aligned run of 32 entries (the blocks of one seq index in the prefill layout) names every decode device exactly once. `queries`: the new token's query entries, real-valued.
All inputs are finite; a program needn't handle non-finite values.
Results may differ from a plain program's by a relative error of at most 0.001.
Values may be sent and summed in bfloat16 or wider, within the bound.
No kernel may reach another device: no remote copies, remote signals or barrier semaphores. Data moves between devices by JAX's collectives and lax.ppermute only.
A program may use at most 64 MiB of HBM per device.

v0:
```python
import jax
import jax.numpy as jnp
from jax import lax
from jax.sharding import PartitionSpec as P


def joined(x, axis, combine):
    everything = jax.tree.map(lambda part: lax.all_gather(part, axis), x)
    leading = jax.tree.map(lambda part: part[0], everything)

    def lap(k, so_far):
        return combine(so_far, jax.tree.map(lambda part: part[k], everything))

    return lax.fori_loop(1, lax.axis_size(axis), lap, leading)


def combine(first, second):
    largest = jnp.maximum(first[0], second[0])
    factor_a = jnp.exp(first[0] - largest)
    factor_b = jnp.exp(second[0] - largest)
    totals = first[1] * factor_a + second[1] * factor_b
    accum = first[2] * factor_a[..., None] + second[2] * factor_b[..., None]
    return (largest, totals, accum)


def slot_info(global_ids, lengths, block_len, blk_seq, batch):
    seq_ids = global_ids // blk_seq
    starts = global_ids % blk_seq * block_len
    positions = starts[:, None] + jnp.arange(block_len, dtype=jnp.int32)[None, :]
    seq_hot = (seq_ids[:, None] == jnp.arange(batch, dtype=jnp.int32)[None, :]).astype(jnp.int32)
    slot_len = jnp.sum(seq_hot * lengths[None, :], axis=1)
    live = positions < slot_len[:, None]
    return (seq_hot, live)


def partials(cache, key_map, value_map, slot_query, live, seq_hot):
    rank = cache.shape[3] // 2
    head_dim = slot_query.shape[-1]
    scale = 1.0 / float(head_dim) ** 0.5
    highest = lax.Precision.HIGHEST
    key_lat = cache[..., :rank]
    value_lat = cache[..., rank:]
    keys = jnp.einsum("gstr,grkd->gstkd", key_lat, key_map, preferred_element_type=jnp.float32)
    scores = (
        jnp.einsum("gstkd,sgkjd->gskjt", keys, slot_query.astype(jnp.float32), precision=highest)
        * scale
    )
    live_wide = live[None, :, None, None, :]
    scores = jnp.where(live_wide, scores, -1e30)
    slot_max = jnp.max(scores, axis=-1)
    weights = jnp.where(live_wide, jnp.exp(scores - slot_max[..., None]), 0.0)
    slot_tot = jnp.sum(weights, axis=-1)
    values = jnp.einsum(
        "gstr,grkd->gstkd", value_lat, value_map, preferred_element_type=jnp.float32
    )
    slot_acc = jnp.einsum("gskjt,gstkd->gskjd", weights, values, precision=highest)
    hot_bool = seq_hot > 0
    hot_float = seq_hot.astype(jnp.float32)
    spread = jnp.where(hot_bool[None, :, None, None, :], slot_max[..., None], -1e30)
    seq_max = jnp.max(spread, axis=1)
    slot_seq_max = jnp.sum(
        jnp.where(hot_bool[None, :, None, None, :], seq_max[:, None], 0.0), axis=-1
    )
    factor = jnp.exp(slot_max - slot_seq_max)
    totals = jnp.einsum("gskj,sb->gkjb", slot_tot * factor, hot_float, precision=highest)
    accum = jnp.einsum(
        "gskjd,sb->gkjbd", slot_acc * factor[..., None], hot_float, precision=highest
    )
    return (seq_max, totals, accum)


def body(latent, up_key, up_value, queries, lengths, block_dest):
    groups = up_key.shape[0]
    dests = latent.shape[1]
    block_len = latent.shape[2]
    rank = latent.shape[3] // 2
    shards = block_dest.shape[0] // dests
    batch = queries.shape[0]
    q_heads = queries.shape[1]
    head_dim = queries.shape[2]
    per_group = up_key.shape[2] // head_dim
    per_kv = q_heads // (groups * per_group)
    blk_seq = block_dest.shape[0] // batch
    own_shard = lax.axis_index("seq")
    own_dests = lax.dynamic_slice_in_dim(block_dest, own_shard * dests, dests)
    source_order = (
        jnp.zeros((dests,), jnp.int32).at[own_dests].set(jnp.arange(dests, dtype=jnp.int32))
    )
    outgoing = latent[0][source_order]
    received = lax.all_to_all(outgoing, ("grp", "seq"), split_axis=0, concat_axis=0, tiled=True)
    received = received.reshape(groups, shards, block_len, 2 * rank)
    decode_latent = received[None]
    key_map = up_key.reshape(groups, rank, per_group, head_dim)
    value_map = up_value.reshape(groups, rank, per_group, head_dim)
    query_rows = queries.reshape(batch, q_heads * head_dim)
    own_group = lax.axis_index("grp")
    slots = latent.shape[1]
    global_ids = own_shard * slots + jnp.arange(slots, dtype=jnp.int32)
    seq_hot, live = slot_info(global_ids, lengths, block_len, blk_seq, batch)
    picked = jnp.dot(seq_hot.astype(jnp.bfloat16), query_rows, preferred_element_type=jnp.float32)
    slot_query = picked.astype(jnp.bfloat16).reshape(slots, groups, per_group, per_kv, head_dim)
    group_query = lax.dynamic_slice_in_dim(slot_query, own_group, 1, 1)
    group_key = lax.dynamic_slice_in_dim(key_map, own_group, 1, 0)
    group_value = lax.dynamic_slice_in_dim(value_map, own_group, 1, 0)
    local = partials(latent, group_key, group_value, group_query, live, seq_hot)
    merged = joined(local, "seq", combine)
    part_result = merged[2] / merged[1][..., None]
    result = lax.all_gather(part_result, "grp", axis=0, tiled=True)
    attended = jnp.transpose(result, (3, 0, 1, 2, 4)).reshape(batch, q_heads * head_dim)
    return (decode_latent, attended)


def solution(mesh):
    return jax.shard_map(
        body,
        mesh=mesh,
        in_specs=(P("grp", "seq", None, None), P(), P(), P(), P(), P()),
        out_specs=(P(("grp", "seq"), None, None, None, None), P()),
        check_vma=False,
    )
```

profile of v0, /device:TPU:0, one launch (start us, length us, event | category | flops | bytes accessed | tf_op | source)
XLA Modules:
  0.0 64.5 jit_solution(13679540145000248874)
XLA Ops:
  0.6 0.0 copy-start.4
  0.6 0.7 %copy-done.4 = s32[256]{0:T(256)S(1)} copy-done((s32[256]{0:T(256)S(1)}, s32[256]{0:T(256)}, u32[]{:S(2)}) %copy-start.4) | copy-done | bytes 1048
  1.3 0.1 compare_select_fusion.1
  1.4 0.7 %scatter_custom_fusion = s32[32]{0:T(128)S(1)} fusion(s32[32]{0:T(128)S(1)} %compare_select_fusion.1, s32[32]{0:T(128)S(1)} %iota.27, s32[]{:T(128)} %constant.75.clone.1), kind=kCustom, calls=%fused_computation.69 | custom fusion | bytes 132 | tf_op jit(solution)/shard_map/scatter | solution.py:87
  2.1 2.4 %gather_fusion = bf16[32,32,256]{2,1,0:T(8,128)(2,1)} fusion(bf16[32,32,256]{2,1,0:T(8,128)(2,1)} %bitcast.100, s32[1024]{0:T(1024)S(1)} %pad_clamp_fusion), kind=kCustom, calls=%fused_computation | custom fusion | bytes 1048704 | tf_op jit(solution)/shard_map/gather | solution.py:89
  4.5 0.0 copy-start.1
  4.5 7.3 %all-to-all-start = ((bf16[32,32,256]{2,1,0:T(8,128)(2,1)}), bf16[32,32,256]{2,1,0:T(8,128)(2,1)S(1)}, u32[]{:S(2)}, u32[]{:S(2)}) async-start(bf16[32,32,256]{2,1,0:T(8,128)(2,1)} %gather_fusion), calls=%async_computation | async-start | bytes 1048576 | tf_op jit(solution)/shard_map/all_to_all | solution.py:90
  11.9 0.0 copy-start.5
  11.9 0.6 copy-done.5
  12.5 0.1 select_reduce_fusion.2
  12.6 0.0 copy-done.1
  12.6 0.0 copy-start.2
  12.6 0.1 reshape.227
  12.7 0.9 %copy-done.2 = bf16[4,128,256]{2,1,0:T(8,128)(2,1)S(1)} copy-done((bf16[4,128,256]{2,1,0:T(8,128)(2,1)S(1)}, bf16[4,128,256]{2,1,0:T(8,128)(2,1)}, u32[]{:S(2)}) %copy-start.2) | copy-done | bytes 262168
  13.6 0.0 copy-start
  13.6 0.1 reshape.230
  13.6 0.1 constant_dynamic-slice_fusion
  13.7 0.9 %copy-done = bf16[1,32,32,256]{3,2,1,0:T(8,128)(2,1)S(1)} copy-done((bf16[1,32,32,256]{3,2,1,0:T(8,128)(2,1)S(1)}, bf16[1,32,32,256]{3,2,1,0:T(8,128)(2,1)}, u32[]{:S(2)}) %copy-start) | copy-done | bytes 524312
  14.6 0.0 copy-start.3
  14.6 0.3 convolution_bitcast_fusion.1
  14.9 0.6 copy-done.3
  15.5 0.3 fusion.5
  15.9 0.1 copy.47
  16.0 0.1 add_compare_fusion
  16.1 1.1 %fusion.35 = (f32[32,2,8]{2,1,0:T(2,128)S(1)}, f32[32,2,8,32]{3,2,1,0:T(8,128)S(1)}) fusion(f32[32,32,2,128]{3,1,2,0:T(8,128)S(1)} %convolution_bitcast_fusion.1, bf16[32,4,2,8,128]{4,3,2,1,0:T(8,128)(2,1)S(1)} %bitcast.103, s32[]{:T(128)S(6)} %select_n.84, pred[32,32]{1,0:T(8,128)(4,1)S(1)} %add_compare_fusion), kind=kOutput, calls=%fused_computation.72 | convolution fusion | flops 25214464 | bytes 1251332 | tf_op jit(solution)/shard_map/gstkd,sgkjd->gskjt/dot_general | solution.py:45
  17.1 0.1 copy.31
  17.2 0.1 select_reduce_fusion.1
  17.3 0.1 select_reduce_fusion
  17.4 9.8 %all-gather = f32[16,8,8]{2,1,0:T(8,128)S(1)} all-gather(f32[2,8,8]{2,1,0:T(8,128)S(1)} %select_reduce_fusion.1), channel_id=2, replica_groups=mesh['grp'=4,'seq'=8] {'seq'}, dimensions={0}, use_global_device_ids=true | all-gather | bytes 4608 | tf_op jit(solution)/shard_map/all_gather | solution.py:8
  27.2 0.1 copy.36
  27.3 0.3 convolution_bitcast_fusion
  27.6 0.3 fusion.13
  27.8 1.1 %convolution_multiply_fusion = f32[32,2,8,128]{3,2,1,0:T(8,128)S(1)} fusion(f32[32,32,2,128]{3,1,0,2:T(8,128)S(1)} %convolution_bitcast_fusion, f32[32,2,8,32]{3,2,1,0:T(8,128)S(1)} %get-tuple-element.228, f32[32,2,8]{2,1,0:T(2,128)S(1)} %copy.36, f32[32,2,8]{2,1,0:T(2,128)S(1)} %get-tuple-element.227, pred[32,32]{1,0:T(8,128)(4,1)S(1)} %add_compare_fusion), kind=kOutput, calls=%fused_computation.16 | convolution fusion | flops 25264128 | bytes 1381376 | tf_op jit(solution)/shard_map/gskjt,gstkd->gskjd/dot_general | solution.py:56
  28.9 0.3 convolution_bitcast_fusion.2
  29.2 9.7 %all-gather.2 = f32[8,2,8,8,128]{4,3,2,1,0:T(8,128)S(1)} all-gather(f32[1,2,8,8,128]{4,3,2,1,0:T(8,128)S(1)} %convolution_bitcast_fusion.2), channel_id=4, replica_groups=mesh['grp'=4,'seq'=8] {'seq'}, dimensions={0}, use_global_device_ids=true | all-gather | bytes 589824 | tf_op jit(solution)/shard_map/all_gather | solution.py:8
  38.9 0.1 copy.33
  39.0 0.1 fusion.21
  39.1 8.4 %all-gather.1 = f32[16,8,8]{2,1,0:T(8,128)S(1)} all-gather(f32[2,8,8]{2,1,0:T(8,128)S(1)} %fusion.21), channel_id=3, replica_groups=mesh['grp'=4,'seq'=8] {'seq'}, dimensions={0}, use_global_device_ids=true | all-gather | bytes 4608 | tf_op jit(solution)/shard_map/all_gather | solution.py:8
  47.5 1.4 %while.19 = (s32[]{:T(128)}, f32[1,2,8,8]{3,2,1,0:T(8,128)S(1)}, f32[1,2,8,8]{3,2,1,0:T(8,128)S(1)}, f32[1,2,8,8,128]{4,3,2,1,0:T(8,128)S(1)}, f32[8,1,2,8,8]{4,...) while((s32[]{:T(128)}, f32[1,2,8,8]{3,2,1,0:T(8,128)S(1)}, ...), condition=%wide.region_7.8_spmd, body=%wide.region_6.7_spmd.sunk | while | flops 50053 | bytes 204443 | solution.py:14
  47.6 0.1 fusion.42
  47.7 0.1 fusion.42
  47.9 0.1 fusion.42
  48.1 0.1 fusion.42
  48.3 0.1 fusion.42
  48.5 0.1 fusion.42
  48.7 0.1 fusion.42
  48.9 0.1 broadcast_divide_fusion
  49.0 14.0 %all_gather.27 = f32[4,2,8,8,128]{4,3,2,1,0:T(8,128)S(1)} all-gather(f32[1,2,8,8,128]{4,3,2,1,0:T(8,128)S(1)} %broadcast_divide_fusion), channel_id=1, replica_groups=mesh['grp'=4,'seq'=8] {'grp'}, dimensions={0}, use_global_device_ids=true | all-gather | bytes 327680 | tf_op jit(solution)/shard_map/all_gather | solution.py:108
  63.0 0.0 all-to-all-done
  63.0 0.8 %copy.74 = bf16[1,4,8,32,256]{4,3,2,1,0:T(8,128)(2,1)} copy(bf16[1,4,8,32,256]{4,3,2,1,0:T(8,128)(2,1)S(1)} %bitcast.99) | data formatting | bytes 1048576
  63.8 0.7 %copy.75 = f32[8,8192]{1,0:T(8,128)} copy(f32[8,8192]{1,0:T(8,128)S(1)} %bitcast.102) | data formatting | bytes 524288
  (30 shorter events, 0.3 us)
Async XLA Ops:
  0.6 0.7 %copy-start.4 = (s32[256]{0:T(256)S(1)}, s32[256]{0:T(256)}, u32[]{:S(2)}) copy-start(s32[256]{0:T(256)} %param.13) | copy-start | bytes 3076
  4.5 8.1 %copy-start.1 = (bf16[4,128,256]{2,1,0:T(8,128)(2,1)S(1)}, bf16[4,128,256]{2,1,0:T(8,128)(2,1)}, u32[]{:S(2)}) copy-start(bf16[4,128,256]{2,1,0:T(8,128)(2,1)} %param.9) | copy-start | bytes 786436
  4.5 58.4 %all-to-all-start = ((bf16[32,32,256]{2,1,0:T(8,128)(2,1)}), bf16[32,32,256]{2,1,0:T(8,128)(2,1)S(1)}, u32[]{:S(2)}, u32[]{:S(2)}) async-start(bf16[32,32,256]{2,1,0:T(8,128)(2,1)} %gather_fusion), calls=%async_computation | async-start | bytes 1048576 | tf_op jit(solution)/shard_map/all_to_all | solution.py:90
  11.9 0.7 %copy-start.5 = (s32[8]{0:T(128)S(1)}, s32[8]{0:T(128)}, u32[]{:S(2)}) copy-start(s32[8]{0:T(128)} %param.12) | copy-start | bytes 100
  12.6 1.0 %copy-start.2 = (bf16[4,128,256]{2,1,0:T(8,128)(2,1)S(1)}, bf16[4,128,256]{2,1,0:T(8,128)(2,1)}, u32[]{:S(2)}) copy-start(bf16[4,128,256]{2,1,0:T(8,128)(2,1)} %param.10) | copy-start | bytes 786436
  13.6 1.0 %copy-start = (bf16[1,32,32,256]{3,2,1,0:T(8,128)(2,1)S(1)}, bf16[1,32,32,256]{3,2,1,0:T(8,128)(2,1)}, u32[]{:S(2)}) copy-start(bf16[1,32,32,256]{3,2,1,0:T(8,128)(2,1)} %param.8) | copy-start | bytes 1572868
  14.6 0.9 %copy-start.3 = (bf16[8,64,128]{2,1,0:T(8,128)(2,1)S(1)}, bf16[8,64,128]{2,1,0:T(8,128)(2,1)}, u32[]{:S(2)}) copy-start(bf16[8,64,128]{2,1,0:T(8,128)(2,1)} %param.11) | copy-start | bytes 393220
where the time goes:
time: 64.9 us; the launch traced here: 64.5 us
  blocking collectives  41.9 us (65%)
  local copies, waits for them, and re-layouts  8.87 us (14%)
  starting transfers between devices  7.33 us (11%)
  matrix products  3.45 us (5%)
  other arithmetic  1.85 us (3%)
  between operations  0.79 us (1%)
    all_gather x3, blocking collectives, joined(): everything = jax.tree.map(lambda part: lax.all_gather(part, axis), x)  27.9 us
    all_gather x1, blocking collectives, body(): result = lax.all_gather(part_result, 'grp', axis=0, tiled=True)  14 us
    all_to_all x1, starting transfers between devices, body(): lax.all_to_all(outgoing, ('grp', 'seq'), split_axis=0, concat_axis=0, til...  7.33 us
    unnamed x15, local copies, waits for them, and re-layouts  5.29 us
    gather x1, local copies, waits for them, and re-layouts, body(): outgoing = latent[0][source_order]  2.42 us
  transfers between devices with their start and end apart: 1, of which 0 were waited for; matrix products, arithmetic and copies ran while one was open for 9% of the time, Pallas kernels for 0%

commit v1 on v0

v1 whole, which is shorter than its diff:
```python
import functools

import jax
import jax.numpy as jnp
from jax import lax
from jax.experimental import pallas as pl
from jax.experimental.pallas import tpu as pltpu
from jax.sharding import PartitionSpec as P


AXES = ("grp", "seq")
F32 = jnp.float32
BF16 = jnp.bfloat16


def three_parts(x):
    high = x.astype(BF16)
    rest = x - high.astype(F32)
    middle = rest.astype(BF16)
    low = (rest - middle.astype(F32)).astype(BF16)
    return jnp.concatenate([high, middle, low], axis=0)


def exact_dot(x, y, contract):
    rows = x.shape[0]
    wide = lax.dot_general(
        three_parts(x), y, ((contract), ((), ())), preferred_element_type=F32
    )
    return wide[:rows] + (wide[rows : 2 * rows] + wide[2 * rows :])


def relayout_kernel(dest_hbm, lat_hbm, out_ref, nat_ref, dest_smem, sems):
    slots = lat_hbm.shape[0]
    first = lax.axis_index("seq") * slots
    get_dest = pltpu.make_async_copy(dest_hbm, dest_smem, sems.at[0])
    get_lat = pltpu.make_async_copy(lat_hbm, nat_ref, sems.at[1])
    get_dest.start()
    get_lat.start()
    get_dest.wait()
    get_lat.wait()

    def move(j, carry):
        out_ref[dest_smem[first + j]] = nat_ref[j]
        return carry

    lax.fori_loop(0, slots, move, 0, unroll=8)


def relayout(block_dest, latent):
    return pl.pallas_call(
        relayout_kernel,
        out_shape=(
            jax.ShapeDtypeStruct(latent.shape, latent.dtype),
            jax.ShapeDtypeStruct(latent.shape, latent.dtype),
        ),
        in_specs=[pl.BlockSpec(memory_space=pl.ANY)] * 2,
        out_specs=(pl.BlockSpec(memory_space=pltpu.VMEM),) * 2,
        scratch_shapes=[
            pltpu.SMEM(block_dest.shape, jnp.int32),
            pltpu.SemaphoreType.DMA((2,)),
        ],
        name="relayout",
    )(block_dest, latent)


def attend_kernel(per_seq, block_len, lat_ref, key_ref, value_ref, query_ref, length_ref, *outs):
    slots = lat_ref.shape[0]
    rank = lat_ref.shape[2] // 2
    head_dim = query_ref.shape[2]
    per_group = key_ref.shape[2] // head_dim
    heads = query_ref.shape[1] // key_ref.shape[0]
    per_kv = heads // per_group
    scale = 1.0 / float(head_dim) ** 0.5
    group = lax.axis_index("grp")
    block = lax.axis_index("seq") * slots
    seq = block // per_seq
    start = (block % per_seq) * block_len
    length = length_ref[seq]
    tokens = slots * block_len
    lat = lat_ref[...].reshape(tokens, 2 * rank)
    query = query_ref[seq, pl.ds(pl.multiple_of(group * heads, heads), heads), :]
    absorbed = []
    for k in range(per_group):
        q = query[k * per_kv : (k + 1) * per_kv]
        u = key_ref[group, :, k * head_dim : (k + 1) * head_dim]
        absorbed.append(
            lax.dot_general(q, u, (((1,), (1,)), ((), ())), preferred_element_type=F32)
        )
    absorbed = jnp.concatenate(absorbed, axis=0)
    scores = exact_dot(absorbed, lat[:, :rank], ((1,), (1,))) * scale
    position = start + lax.broadcasted_iota(jnp.int32, scores.shape, 1)
    live = position < length
    scores = jnp.where(live, scores, -1e30)
    top = jnp.max(scores, axis=1, keepdims=True)
    weights = jnp.where(live, jnp.exp(scores - top), 0.0)
    total = jnp.sum(weights, axis=1, keepdims=True)
    mixed = exact_dot(weights, lat[:, rank:], ((1,), (0,)))
    attended = []
    for k in range(per_group):
        u = value_ref[group, :, k * head_dim : (k + 1) * head_dim]
        attended.append(exact_dot(mixed[k * per_kv : (k + 1) * per_kv], u, ((1,), (0,))))
    attended = jnp.concatenate(attended, axis=0)
    (out_ref,) = outs
    if out_ref.shape[1] == heads:
        rows = attended / total
    else:
        rows = jnp.concatenate(
            [attended, jnp.broadcast_to(top, attended.shape), jnp.broadcast_to(total, attended.shape)],
            axis=0,
        )
    for d in range(out_ref.shape[0]):
        out_ref[d] = rows


def attend(latent, up_key, up_value, queries, lengths, dests, spans, per_seq):
    heads = queries.shape[1] // up_key.shape[0]
    rows = heads if spans == 1 else 3 * heads
    vmem = pl.BlockSpec(memory_space=pltpu.VMEM)
    return pl.pallas_call(
        functools.partial(attend_kernel, per_seq, latent.shape[1]),
        out_shape=jax.ShapeDtypeStruct((dests, rows, queries.shape[2]), F32),
        in_specs=[vmem] * 4 + [pl.BlockSpec(memory_space=pltpu.SMEM)],
        out_specs=vmem,
        name="attend",
    )(latent, up_key, up_value, queries, lengths)


def gathered_by_pairs(x, axis):
    size = lax.axis_size(axis)
    step = 1
    while step < size:
        pairs = [[i, i + step] for i in range(size) if not i & step]
        x = lax.all_gather(x, axis, axis=0, tiled=True, axis_index_groups=pairs)
        step *= 2
    return x


def body(latent, up_key, up_value, queries, lengths, block_dest):
    groups = up_key.shape[0]
    slots = latent.shape[1]
    batch = queries.shape[0]
    heads = queries.shape[1] // groups
    head_dim = queries.shape[2]
    per_seq = block_dest.shape[0] // batch
    shards = lax.axis_size("seq")
    spans = per_seq // slots
    assert spans * slots == per_seq and spans * batch == shards

    outgoing, natural = relayout(block_dest, latent[0])
    received = lax.all_to_all(outgoing, AXES, split_axis=0, concat_axis=0, tiled=True)
    decode_latent = received.reshape((1, groups, shards) + latent.shape[2:])

    mine = attend(natural, up_key, up_value, queries, lengths, 1, spans, per_seq)
    mine = gathered_by_pairs(mine, "grp")
    every = lax.all_gather(mine, "seq", axis=0)
    every = jnp.swapaxes(every, 0, 1)
    every = every.reshape(groups, batch, spans, -1, head_dim)
    if spans == 1:
        result = every[:, :, 0]
    else:
        accum, top, total = (every[:, :, :, k * heads : (k + 1) * heads] for k in range(3))
        factor = jnp.exp(top - jnp.max(top, axis=2, keepdims=True))
        result = jnp.sum(accum * factor, axis=2) / jnp.sum(total * factor, axis=2)
    attended = jnp.transpose(result, (1, 0, 2, 3)).reshape(batch, groups * heads * head_dim)
    return (decode_latent, attended)


def solution(mesh):
    return jax.shard_map(
        body,
        mesh=mesh,
        in_specs=(P("grp", "seq", None, None), P(), P(), P(), P(), P()),
        out_specs=(P(AXES, None, None, None, None), P()),
        check_vma=False,
    )
```

time: 64.9 us -> 37.4 us (0.58)
  blocking collectives: 41.9 us -> 23 us
  local copies, waits for them, and re-layouts: 8.87 us -> 1.55 us
  Pallas kernels: 0 us -> 4.62 us
  matrix products: 3.45 us -> 0 us
  other arithmetic: 1.85 us -> 0 us
    all_gather x4 -> x3, blocking collectives: 41.9 us -> 23 us  [the longest x2 13.7 us: gathered_by_pairs(): x = lax.all_gather(x, axis, axis=0, tiled=True, axis_index_groups=pairs)]
    pallas_call x0 -> x2, Pallas kernels: none -> 4.62 us  [the longest x1 2.53 us: attend(): pl.pallas_call(functools.partial(attend_kernel, per_seq, latent.shape[1])...]
    unnamed x15 -> x1, local copies, waits for them, and re-layouts: 5.29 us -> 0.79 us
    dot_general x7 -> x0, matrix products: 3.45 us -> none  [the longest x1 1.05 us: partials(): jnp.einsum('gstkd,sgkjd->gskjt', keys, slot_query.astype(jnp.float32), pr...]
    gather x1 -> x0, local copies, waits for them, and re-layouts: 2.42 us -> none  [body(): outgoing = latent[0][source_order]]
    add x7 -> x0, other arithmetic: 0.8 us -> none  [combine(): accum = first[2] * factor_a[..., None] + second[2] * factor_b[..., None]]
    scatter x1 -> x0, local copies, waits for them, and re-layouts: 0.67 us -> none  [body(): jnp.zeros((dests,), jnp.int32).at[own_dests]]
  transfers between devices with their start and end apart: 1 -> 1, of which waited for: 0 -> 0; matrix products, arithmetic and copies ran while one was open for 9% -> 2% of each run, Pallas kernels for 0% -> 7%
where the time goes in v1:
time: 37.4 us; the launch traced here: 37.1 us
  blocking collectives  23 us (61%)
  starting transfers between devices  7.33 us (20%)
  Pallas kernels  4.62 us (12%)
  local copies, waits for them, and re-layouts  1.55 us (4%)
  between operations  0.65 us (2%)
    all_gather x2, blocking collectives, gathered_by_pairs(): x = lax.all_gather(x, axis, axis=0, tiled=True, axis_index_groups=pairs)  13.7 us
    all_gather x1, blocking collectives, body(): every = lax.all_gather(mine, 'seq', axis=0)  9.27 us
    all_to_all x1, starting transfers between devices, body(): lax.all_to_all(outgoing, AXES, split_axis=0, concat_axis=0, tiled=True)  7.33 us
    pallas_call x1, Pallas kernels, attend(): pl.pallas_call(functools.partial(attend_kernel, per_seq, latent.shape[1])...  2.53 us
    pallas_call x1, Pallas kernels, relayout(): pl.pallas_call(relayout_kernel, out_shape=(jax.ShapeDtypeStruct(latent.sh...  2.09 us
    unnamed x1, local copies, waits for them, and re-layouts  0.79 us
    reshape x1, local copies, waits for them, and re-layouts, body(): jnp.transpose(result, (1, 0, 2, 3))  0.75 us
  transfers between devices with their start and end apart: 1, of which 0 were waited for; matrix products, arithmetic and copies ran while one was open for 2% of the time, Pallas kernels for 7%

profile of v1, /device:TPU:0, one launch (start us, length us, event | category | flops | bytes accessed | tf_op | source)
XLA Modules:
  0.0 37.1 jit_solution(8767469191000452815)
XLA Ops:
  0.6 2.1 %relayout.1 = (bf16[32,32,256]{2,1,0:T(8,128)(2,1)}, bf16[32,32,256]{2,1,0:T(8,128)(2,1)}) custom-call(s32[256]{0:T(256)} %dest_hbm.1, bf16[32,32,256]{2,1,0:T(8,128)(2,1)} %bitcast.3), custom_call_target="tpu_custom_call" | custom-call | tf_op jit(solution)/shard_map/relayout/pallas_call | solution.py:50
  2.7 7.3 %all-to-all-start = ((bf16[32,32,256]{2,1,0:T(8,128)(2,1)}), bf16[32,32,256]{2,1,0:T(8,128)(2,1)S(1)}, u32[]{:S(2)}, u32[]{:S(2)}) async-start(bf16[32,32,256]{2,1,0:T(8,128)(2,1)} %get-tuple-element.4), calls=%async_computation | async-start | bytes 1048576 | tf_op jit(solution)/shard_map/all_to_all | solution.py:150
  10.1 2.5 %attend.1 = f32[1,16,128]{2,1,0:T(8,128)} custom-call(bf16[32,32,256]{2,1,0:T(8,128)(2,1)} %get-tuple-element.5.lat_ref, bf16[4,128,256]{2,1,0:T(8,128)(2,1)} %key_ref.1, bf16[4,128,256]{2,1,0:T(8,128)(2,1)} %value_ref.1, bf16[8,64,128]{2,1,0:T(8,128)(2,1)} %query_ref.1, s32[8]{0:T(128)} %length_ref.1), custom_call_target="tpu_custom_call" | custom-call | tf_op jit(solution)/shard_map/attend/pallas_call | solution.py:119
  12.6 6.8 %all_gather.12 = f32[2,16,128]{2,1,0:T(8,128)S(1)} all-gather(f32[1,16,128]{2,1,0:T(8,128)} %attend.1), channel_id=1, replica_groups={{0,8},{16,24},{1,9},{17,25},{2,10},{18,26},{3,11},{19,27},{4,12},{20,28..., dimensions={0}, use_global_device_ids=true | all-gather | bytes 24576 | tf_op jit(solution)/shard_map/all_gather | solution.py:133
  19.4 6.9 %all_gather.13 = f32[4,16,128]{2,1,0:T(8,128)S(1)} all-gather(f32[2,16,128]{2,1,0:T(8,128)S(1)} %all_gather.12), channel_id=1, replica_groups={{0,16},{8,24},{1,17},{9,25},{2,18},{10,26},{3,19},{11,27},{4,20},{12,28..., dimensions={0}, use_global_device_ids=true | all-gather | bytes 49152 | tf_op jit(solution)/shard_map/all_gather | solution.py:133
  26.3 9.3 %all-gather = f32[32,16,128]{2,1,0:T(8,128)S(1)} all-gather(f32[4,16,128]{2,1,0:T(8,128)S(1)} %all_gather.13), channel_id=2, replica_groups=mesh['grp'=4,'seq'=8] {'seq'}, dimensions={0}, use_global_device_ids=true | all-gather | bytes 294912 | tf_op jit(solution)/shard_map/all_gather | solution.py:155
  35.6 0.8 %reshape.11 = f32[8,8192]{1,0:T(8,128)} reshape(f32[32,16,128]{2,1,0:T(8,128)S(1)} %all-gather) | data formatting | bytes 524288 | tf_op jit(solution)/shard_map/reshape | solution.py:164
  36.3 0.0 all-to-all-done
  36.3 0.8 %copy.9 = bf16[1,4,8,32,256]{4,3,2,1,0:T(8,128)(2,1)} copy(bf16[1,4,8,32,256]{4,3,2,1,0:T(8,128)(2,1)S(1)} %bitcast.2) | data formatting | bytes 1048576
Async XLA Ops:
  2.7 33.6 %all-to-all-start = ((bf16[32,32,256]{2,1,0:T(8,128)(2,1)}), bf16[32,32,256]{2,1,0:T(8,128)(2,1)S(1)}, u32[]{:S(2)}, u32[]{:S(2)}) async-start(bf16[32,32,256]{2,1,0:T(8,128)(2,1)} %get-tuple-element.4), calls=%async_computation | async-start | bytes 1048576 | tf_op jit(solution)/shard_map/all_to_all | solution.py:150

commit v2 on v1

v2 whole, which is shorter than its diff:
```python
import functools
import math

import jax
import jax.numpy as jnp
from jax import lax
from jax.experimental import pallas as pl
from jax.experimental.pallas import tpu as pltpu
from jax.sharding import PartitionSpec as P

AXES = ("grp", "seq")
F32 = jnp.float32
BF16 = jnp.bfloat16
NEAR_BYTES = 1 << 20


def parts_of(x, count):
    parts = []
    for _ in range(count):
        part = x.astype(BF16)
        parts.append(part)
        x = x - part.astype(F32)
    return parts


def exact_dot(x, y, contract):
    rows = x.shape[0]
    wide = lax.dot_general(
        jnp.concatenate(parts_of(x, 3), axis=0),
        y,
        (contract, ((), ())),
        preferred_element_type=F32,
    )
    return wide[:rows] + (wide[rows : 2 * rows] + wide[2 * rows :])


def in_vmem(shape):
    return 2 * math.prod(shape) <= NEAR_BYTES


def start_kernel(
    per_seq,
    sent,
    dest_hbm,
    length_hbm,
    lat_hbm,
    key_hbm,
    value_hbm,
    query_hbm,
    out_ref,
    dest,
    length,
    lat_ref,
    key_ref,
    value_ref,
    query_ref,
    sems,
):
    slots, block_len, width = lat_ref.shape
    rank = width // 2
    heads, head_dim = query_ref.shape
    per_group = key_ref.shape[1] // head_dim
    per_kv = heads // per_group
    scale = 1.0 / float(head_dim) ** 0.5
    group = lax.axis_index("grp")
    first = lax.axis_index("seq") * slots
    seq = first // per_seq
    start = (first % per_seq) * block_len
    rows = pl.ds(pl.multiple_of(group * heads, heads), heads)
    sources = (lat_hbm, dest_hbm, key_hbm.at[group], query_hbm.at[seq, rows], length_hbm, value_hbm.at[group])
    targets = (lat_ref, dest, key_ref, query_ref, length, value_ref)
    copies = [
        pltpu.make_async_copy(source, target, sems.at[k])
        for k, (source, target) in enumerate(zip(sources, targets))
    ]
    for copy in copies:
        copy.start()
    for copy in copies:
        copy.wait()

    def move(j, carry):
        out_ref[dest[first + j], :block_len, :] = lat_ref[j]
        return carry

    lax.fori_loop(0, slots, move, 0, unroll=8)

    tokens = slots * block_len
    lat = lat_ref[...].reshape(tokens, width)
    absorbed = []
    for k in range(per_group):
        columns = slice(k * head_dim, (k + 1) * head_dim)
        absorbed.append(
            lax.dot_general(
                query_ref[k * per_kv : (k + 1) * per_kv, :],
                key_ref[:, columns],
                (((1,), (1,)), ((), ())),
                preferred_element_type=F32,
            )
        )
    absorbed = jnp.concatenate(absorbed, axis=0)
    scores = exact_dot(absorbed, lat[:, :rank], ((1,), (1,))) * scale
    position = start + lax.broadcasted_iota(jnp.int32, scores.shape, 1)
    live = position < length[seq]
    scores = jnp.where(live, scores, -1e30)
    top = jnp.max(scores, axis=1, keepdims=True)
    weights = jnp.where(live, jnp.exp(scores - top), 0.0)
    total = jnp.sum(weights, axis=1, keepdims=True)
    mixed = exact_dot(weights, lat[:, rank:], ((1,), (0,)))
    if per_seq == slots:
        mixed = mixed / total
    attended = []
    for k in range(per_group):
        columns = slice(k * head_dim, (k + 1) * head_dim)
        attended.append(
            exact_dot(mixed[k * per_kv : (k + 1) * per_kv], value_ref[:, columns], ((1,), (0,)))
        )
    fields = [jnp.concatenate(attended, axis=1)]
    if per_seq != slots:
        for field in (top, total):
            fields.append(
                jnp.concatenate(
                    [
                        jnp.broadcast_to(field[k * per_kv : (k + 1) * per_kv], (per_kv, head_dim))
                        for k in range(per_group)
                    ],
                    axis=1,
                )
            )
    extra = jnp.concatenate([part for field in fields for part in parts_of(field, sent)], axis=0)
    for d in range(out_ref.shape[0]):
        out_ref[d, block_len:, :] = extra


def start(latent, up_key, up_value, queries, lengths, block_dest, dests, extra_rows, sent):
    slots, block_len, width = latent.shape
    batch, q_heads, head_dim = queries.shape
    groups = up_key.shape[0]
    per_seq = block_dest.shape[0] // batch
    shape = (dests, block_len + extra_rows, width)
    near = in_vmem(shape)
    return pl.pallas_call(
        functools.partial(start_kernel, per_seq, sent),
        out_shape=(pltpu.VMEM if near else jax.ShapeDtypeStruct)(shape, latent.dtype),
        in_specs=[pl.BlockSpec(memory_space=pl.ANY)] * 6,
        out_specs=pl.BlockSpec(memory_space=pltpu.VMEM),
        scratch_shapes=[
            pltpu.SMEM(block_dest.shape, jnp.int32),
            pltpu.SMEM(lengths.shape, jnp.int32),
            pltpu.VMEM(latent.shape, latent.dtype),
            pltpu.VMEM(up_key.shape[1:], up_key.dtype),
            pltpu.VMEM(up_value.shape[1:], up_value.dtype),
            pltpu.VMEM((q_heads // groups, head_dim), queries.dtype),
            pltpu.SemaphoreType.DMA((6,)),
        ],
        name="start",
    )(block_dest, lengths, latent, up_key, up_value, queries)


def finish_kernel(spans, sent, head_dim, got_ref, decode_hbm, result_hbm, result_ref, wide_ref, sems):
    block_len = decode_hbm.shape[1]
    batch, columns = result_ref.shape
    copy_blocks = pltpu.make_async_copy(got_ref.at[:, :block_len, :], decode_hbm, sems.at[0])
    copy_blocks.start()
    width = got_ref.shape[2]
    per_group = width // head_dim
    fields = 1 if spans == 1 else 3
    per_kv = (got_ref.shape[1] - block_len) // (sent * fields)
    groups = got_ref.shape[0] // (batch * spans)

    def field(source, k):
        begin = block_len + k * sent * per_kv
        return sum(
            got_ref[source, begin + p * per_kv : begin + (p + 1) * per_kv, :].astype(F32)
            for p in reversed(range(sent))
        )

    for g in range(groups):
        for b in range(batch):
            sources = [(g * batch + b) * spans + k for k in range(spans)]
            if spans == 1:
                value = field(sources[0], 0)
            else:
                tops = [field(source, 1) for source in sources]
                top = functools.reduce(jnp.maximum, tops)
                factors = [jnp.exp(t - top) for t in tops]
                total = sum(field(source, 2) * f for source, f in zip(sources, factors))
                value = sum(field(source, 0) * f for source, f in zip(sources, factors)) / total
            wide_ref[g, b] = value
    for g in range(groups):
        for k in range(per_group):
            for j in range(per_kv):
                column = ((g * per_group + k) * per_kv + j) * head_dim
                result_ref[:, column : column + head_dim] = wide_ref[
                    g, :, j, k * head_dim : (k + 1) * head_dim
                ]
    copy_result = pltpu.make_async_copy(result_ref, result_hbm, sems.at[1])
    copy_result.start()
    copy_blocks.wait()
    copy_result.wait()


def finish(got, block_len, batch, columns, head_dim, spans, sent):
    dests, rows, width = got.shape
    groups = dests // (batch * spans)
    per_kv = columns // (groups * width)
    if in_vmem(got.shape):
        got = pltpu.with_memory_space_constraint(got, pltpu.VMEM)
    return pl.pallas_call(
        functools.partial(finish_kernel, spans, sent, head_dim),
        out_shape=(
            jax.ShapeDtypeStruct((dests, block_len, width), got.dtype),
            jax.ShapeDtypeStruct((batch, columns), F32),
        ),
        in_specs=[pl.BlockSpec(memory_space=pltpu.VMEM)],
        out_specs=(pl.BlockSpec(memory_space=pl.ANY),) * 2,
        scratch_shapes=[
            pltpu.VMEM((batch, columns), F32),
            pltpu.VMEM((groups, batch, per_kv, width), F32),
            pltpu.SemaphoreType.DMA((2,)),
        ],
        name="finish",
    )(got)


def body(latent, up_key, up_value, queries, lengths, block_dest):
    groups = up_key.shape[0]
    slots, block_len, width = latent.shape[1:]
    batch, q_heads, head_dim = queries.shape
    shards = lax.axis_size("seq")
    dests = groups * shards
    spans = shards // batch
    assert spans * batch == shards and up_key.shape[2] == width
    sent, fields = (2, 1) if spans == 1 else (3, 3)
    per_kv = q_heads * head_dim // (groups * width)
    payload = start(
        latent[0], up_key, up_value, queries, lengths, block_dest, dests, sent * fields * per_kv, sent
    )
    got = lax.all_to_all(payload, AXES, split_axis=0, concat_axis=0, tiled=True)
    decode, attended = finish(got, block_len, batch, q_heads * head_dim, head_dim, spans, sent)
    return (decode.reshape(1, groups, shards, block_len, width), attended)


def solution(mesh):
    return jax.shard_map(
        body,
        mesh=mesh,
        in_specs=(P("grp", "seq", None, None), P(), P(), P(), P(), P()),
        out_specs=(P(AXES, None, None, None, None), P()),
        check_vma=False,
    )
```

time: 37.4 us -> 31.3 us (0.84)
  starting transfers between devices: 7.33 us -> 0 us
  blocking collectives: 23 us -> 27.7 us
  Pallas kernels: 4.62 us -> 2.79 us
  local copies, waits for them, and re-layouts: 1.55 us -> 0 us
    all_to_all x0 -> x1, blocking collectives: none -> 27.7 us  [body(): got = lax.all_to_all(payload, AXES, split_axis=0, concat_axis=0, tiled=True)]
    all_gather x3 -> x0, blocking collectives: 23 us -> none  [the longest x2 13.7 us: gathered_by_pairs(): x = lax.all_gather(x, axis, axis=0, tiled=True, axis_index_groups=pairs)]
    all_to_all x1 -> x0, starting transfers between devices: 7.33 us -> none  [body(): lax.all_to_all(outgoing, AXES, split_axis=0, concat_axis=0, tiled=True)]
    pallas_call x2, Pallas kernels: 4.62 us -> 2.79 us  [the longest x1 1.9 us: start(): pl.pallas_call(functools.partial(start_kernel, per_seq, sent), out_shape=...]
    unnamed x1 -> x0, local copies, waits for them, and re-layouts: 0.79 us -> none
    reshape x1 -> x0, local copies, waits for them, and re-layouts: 0.75 us -> none  [body(): jnp.transpose(result, (1, 0, 2, 3))]
  transfers between devices with their start and end apart: 1 -> 0, of which waited for: 0 -> 0; matrix products, arithmetic and copies ran while one was open for 2% -> 0% of each run, Pallas kernels for 7% -> 0%
where the time goes in v2:
time: 31.3 us; the launch traced here: 31.2 us
  blocking collectives  27.7 us (88%)
  Pallas kernels  2.79 us (9%)
  between operations  0.64 us (2%)
    all_to_all x1, blocking collectives, body(): got = lax.all_to_all(payload, AXES, split_axis=0, concat_axis=0, tiled=True)  27.7 us
    pallas_call x1, Pallas kernels, start(): pl.pallas_call(functools.partial(start_kernel, per_seq, sent), out_shape=...  1.9 us
    pallas_call x1, Pallas kernels, finish(): pl.pallas_call(functools.partial(finish_kernel, spans, sent, head_dim), o...  0.89 us

profile of v2, /device:TPU:0, one launch (start us, length us, event | category | flops | bytes accessed | tf_op | source)
XLA Modules:
  0.0 31.2 jit_solution(5959897090444229726)
XLA Ops:
  0.6 1.9 %start.1 = bf16[32,48,256]{2,1,0:T(8,128)(2,1)S(1)} custom-call(s32[256]{0:T(256)} %dest_hbm.1, s32[8]{0:T(128)} %length_hbm.1, bf16[32,32,256]{2,1,0:T(8,128)(2,1)} %bitcast.2, bf16[4,128,256]{2,1,0:T(8,128)(2,1)} %key_hbm.1, bf16[4,128,256]{2,1,0:T(8,128)(2,1)} %value_hbm.1, bf16[8,64,128]{2,1,0:T(8,128)(2,1)} %query_hbm.1), custom_call_target="tpu_custom_call" | custom-call | tf_op jit(solution)/shard_map/start/pallas_call | solution.py:141
  2.5 27.7 %all_to_all.5.got_ref = bf16[32,48,256]{2,1,0:T(8,128)(2,1)S(1)} all-to-all(bf16[32,48,256]{2,1,0:T(8,128)(2,1)S(1)} %start.1), channel_id=1, replica_groups=mesh['grp'=4,'seq'=8] {'grp','seq'}, dimensions={0} | all-to-all | bytes 1572864 | tf_op jit(solution)/shard_map/all_to_all | solution.py:238
  30.3 0.9 %finish.1 = (bf16[32,32,256]{2,1,0:T(8,128)(2,1)}, f32[8,8192]{1,0:T(8,128)}) custom-call(bf16[32,48,256]{2,1,0:T(8,128)(2,1)S(1)} %all_to_all.5.got_ref), custom_call_target="tpu_custom_call" | custom-call | tf_op jit(solution)/shard_map/finish/pallas_call | solution.py:208

commit v3 on v2

v3 whole, which is shorter than its diff:
```python
import functools
import math

import jax
import jax.numpy as jnp
from jax import lax
from jax.experimental import pallas as pl
from jax.experimental.pallas import tpu as pltpu
from jax.sharding import PartitionSpec as P


AXES = ("grp", "seq")
F32 = jnp.float32
BF16 = jnp.bfloat16
NEAR_BYTES = 1 << 20
NEAR_DEVICES = 4


def three_parts(x):
    parts = []
    for _ in range(3):
        part = x.astype(BF16)
        parts.append(part)
        x = x - part.astype(F32)
    return jnp.concatenate(parts, axis=0)


def exact_dot(x, y, contract):
    rows = x.shape[0]
    wide = lax.dot_general(
        three_parts(x),
        y,
        (contract, ((), ())),
        preferred_element_type=F32,
    )
    return wide[:rows] + (wide[rows : 2 * rows] + wide[2 * rows :])


def in_vmem(shape):
    return 4 * math.prod(shape) <= NEAR_BYTES


def start_kernel(
    per_seq,
    dest_hbm,
    length_hbm,
    lat_hbm,
    key_hbm,
    value_hbm,
    query_hbm,
    out_hbm,
    mine_ref,
    dest,
    length,
    lat_ref,
    key_ref,
    value_ref,
    query_ref,
    ordered_ref,
    sems,
):
    slots, block_len, width = lat_ref.shape
    rank = width // 2
    heads, head_dim = query_ref.shape
    per_group = key_ref.shape[1] // head_dim
    per_kv = heads // per_group
    scale = 1.0 / float(head_dim) ** 0.5
    group = lax.axis_index("grp")
    first = lax.axis_index("seq") * slots
    seq = first // per_seq
    start = (first % per_seq) * block_len
    rows = pl.ds(pl.multiple_of(group * heads, heads), heads)
    sources = (lat_hbm, dest_hbm, key_hbm.at[group], query_hbm.at[seq, rows], length_hbm, value_hbm.at[group])
    targets = (lat_ref, dest, key_ref, query_ref, length, value_ref)
    copies = [
        pltpu.make_async_copy(source, target, sems.at[k])
        for k, (source, target) in enumerate(zip(sources, targets))
    ]
    for copy in copies:
        copy.start()
    for copy in copies:
        copy.wait()

    def move(j, carry):
        ordered_ref[dest[first + j]] = lat_ref[j]
        return carry

    lax.fori_loop(0, slots, move, 0, unroll=8)
    send = pltpu.make_async_copy(ordered_ref, out_hbm, sems.at[len(copies)])
    send.start()

    tokens = slots * block_len
    lat = lat_ref[...].reshape(tokens, width)
    absorbed = []
    for k in range(per_group):
        columns = slice(k * head_dim, (k + 1) * head_dim)
        absorbed.append(
            lax.dot_general(
                query_ref[k * per_kv : (k + 1) * per_kv, :],
                key_ref[:, columns],
                (((1,), (1,)), ((), ())),
                preferred_element_type=F32,
            )
        )
    absorbed = jnp.concatenate(absorbed, axis=0)
    scores = exact_dot(absorbed, lat[:, :rank], ((1,), (1,))) * scale
    position = start + lax.broadcasted_iota(jnp.int32, scores.shape, 1)
    live = position < length[seq]
    scores = jnp.where(live, scores, -1e30)
    top = jnp.max(scores, axis=1, keepdims=True)
    weights = jnp.where(live, jnp.exp(scores - top), 0.0)
    total = jnp.sum(weights, axis=1, keepdims=True)
    mixed = exact_dot(weights, lat[:, rank:], ((1,), (0,)))
    if per_seq == slots:
        mixed = mixed / total
    attended = []
    for k in range(per_group):
        columns = slice(k * head_dim, (k + 1) * head_dim)
        attended.append(
            exact_dot(mixed[k * per_kv : (k + 1) * per_kv], value_ref[:, columns], ((1,), (0,)))
        )
    fields = [jnp.concatenate(attended, axis=0)]
    if per_seq != slots:
        fields += [jnp.broadcast_to(field, (heads, head_dim)) for field in (top, total)]
    mine_ref[...] = jnp.concatenate(fields, axis=0)
    send.wait()


def start(latent, up_key, up_value, queries, lengths, block_dest):
    batch, q_heads, head_dim = queries.shape
    heads = q_heads // up_key.shape[0]
    per_seq = block_dest.shape[0] // batch
    rows = heads if per_seq == latent.shape[0] else 3 * heads
    return pl.pallas_call(
        functools.partial(start_kernel, per_seq),
        out_shape=(
            jax.ShapeDtypeStruct(latent.shape, latent.dtype),
            pltpu.VMEM((rows, head_dim), F32),
        ),
        in_specs=[pl.BlockSpec(memory_space=pl.ANY)] * 6,
        out_specs=(pl.BlockSpec(memory_space=pl.ANY), pl.BlockSpec(memory_space=pltpu.VMEM)),
        scratch_shapes=[
            pltpu.SMEM(block_dest.shape, jnp.int32),
            pltpu.SMEM(lengths.shape, jnp.int32),
            pltpu.VMEM(latent.shape, latent.dtype),
            pltpu.VMEM(up_key.shape[1:], up_key.dtype),
            pltpu.VMEM(up_value.shape[1:], up_value.dtype),
            pltpu.VMEM((heads, head_dim), queries.dtype),
            pltpu.VMEM(latent.shape, latent.dtype),
            pltpu.SemaphoreType.DMA((7,)),
        ],
        name="start",
    )(block_dest, lengths, latent, up_key, up_value, queries)


def finish_kernel(groups, shards, offsets, heads, *refs):
    sources, (result_hbm, result_ref, wide_ref, sem) = refs[: len(offsets)], refs[len(offsets) :]
    batch = result_ref.shape[0]
    spans = shards // batch
    near, halves, _, head_dim = sources[0].shape
    group = lax.axis_index("grp")
    major = lax.axis_index("seq") // near
    for (step, flip), source in zip(offsets, sources):
        from_major = (major + step) % (shards // near)
        for half in range(halves):
            from_group = group ^ flip ^ (half * (groups // 2))
            for k in range(near):
                wide_ref[from_group, from_major * near + k] = source[k, half]
    if spans > 1:
        for g in range(groups):
            for b in range(batch):
                parts = [wide_ref[g, b * spans + k] for k in range(spans)]
                accums, tops, totals = (
                    [part[f * heads : (f + 1) * heads] for part in parts] for f in range(3)
                )
                top = functools.reduce(jnp.maximum, tops)
                factors = [jnp.exp(t - top) for t in tops]
                accum = sum(x * f for x, f in zip(accums, factors))
                total = sum(x * f for x, f in zip(totals, factors))
                wide_ref[g, b, :heads] = accum / total
    for g in range(groups):
        for h in range(heads):
            column = (g * heads + h) * head_dim
            result_ref[:, column : column + head_dim] = wide_ref[g, :batch, h, :]
    copy = pltpu.make_async_copy(result_ref, result_hbm, sem)
    copy.start()
    copy.wait()


def finish(pieces, offsets, groups, shards, batch, heads):
    rows, head_dim = pieces[0].shape[2:]
    columns = groups * heads * head_dim
    if in_vmem((len(pieces),) + pieces[0].shape):
        pieces = [pltpu.with_memory_space_constraint(piece, pltpu.VMEM) for piece in pieces]
    return pl.pallas_call(
        functools.partial(finish_kernel, groups, shards, offsets, heads),
        out_shape=jax.ShapeDtypeStruct((batch, columns), F32),
        in_specs=[pl.BlockSpec(memory_space=pltpu.VMEM)] * len(pieces),
        out_specs=pl.BlockSpec(memory_space=pl.ANY),
        scratch_shapes=[
            pltpu.VMEM((batch, columns), F32),
            pltpu.VMEM((groups, shards, rows, head_dim), F32),
            pltpu.SemaphoreType.DMA,
        ],
        name="finish",
    )(*pieces)


def body(latent, up_key, up_value, queries, lengths, block_dest):
    groups = up_key.shape[0]
    _, block_len, width = latent.shape[1:]
    batch, q_heads, _ = queries.shape
    shards = lax.axis_size("seq")
    near = math.gcd(shards, NEAR_DEVICES)
    far = shards // near
    assert groups % 2 == 0 and shards % batch == 0
    payload, mine = start(latent[0], up_key, up_value, queries, lengths, block_dest)
    other = lax.ppermute(mine, "grp", [(i, i ^ (groups // 2)) for i in range(groups)])
    got = lax.all_to_all(payload, AXES, split_axis=0, concat_axis=0, tiled=True)
    both = jnp.stack([mine, other])
    neighbours = [[k * near + i for i in range(near)] for k in range(far)]
    plane = lax.all_gather(both, "seq", axis=0, axis_index_groups=neighbours)
    offsets = [(step, flip) for flip in range(groups // 2) for step in range(far)]
    pieces = [plane]
    for step, flip in offsets[1:]:
        moves = [
            ((g ^ flip) * shards + (s + step * near) % shards, g * shards + s)
            for g in range(groups)
            for s in range(shards)
        ]
        pieces.append(lax.ppermute(plane, AXES, moves))
    attended = finish(pieces, offsets, groups, shards, batch, q_heads // groups)
    return (got.reshape(1, groups, shards, block_len, width), attended)


def solution(mesh):
    return jax.shard_map(
        body,
        mesh=mesh,
        in_specs=(P("grp", "seq", None, None), P(), P(), P(), P(), P()),
        out_specs=(P(AXES, None, None, None, None), P()),
        check_vma=False,
    )
```

time: 31.3 us -> 39.7 us (1.27)
  blocking collectives: 27.7 us -> 5.22 us
  waiting for transfers between devices: 0 us -> 16.3 us
  starting transfers between devices: 0 us -> 13.6 us
  local copies, waits for them, and re-layouts: 0 us -> 0.8 us
    all_to_all x1 -> x0, blocking collectives: 27.7 us -> none  [body(): got = lax.all_to_all(payload, AXES, split_axis=0, concat_axis=0, tiled=True)]
    ppermute x0 -> x4, waiting for transfers between devices: none -> 16.3 us  [the longest x1 12.6 us: body(): lax.ppermute(mine, 'grp', [(i, i ^ groups // 2) for i in range(groups)])]
    all_to_all x0 -> x1, starting transfers between devices: none -> 7.33 us  [body(): got = lax.all_to_all(payload, AXES, split_axis=0, concat_axis=0, tiled=True)]
    ppermute x0 -> x4, starting transfers between devices: none -> 6.23 us  [the longest x3 3.49 us: body(): pieces.append(lax.ppermute(plane, AXES, moves))]
    all_gather x0 -> x1, blocking collectives: none -> 5.22 us  [body(): plane = lax.all_gather(both, 'seq', axis=0, axis_index_groups=neighbours)]
    unnamed x0 -> x1, local copies, waits for them, and re-layouts: none -> 0.8 us
  transfers between devices with their start and end apart: 0 -> 5, of which waited for: 0 -> 4; matrix products, arithmetic and copies ran while one was open for 0% -> 0% of each run, Pallas kernels for 0% -> 2%
where the time goes in v3:
time: 39.7 us; the launch traced here: 39.4 us
  waiting for transfers between devices  16.3 us (41%)
  starting transfers between devices  13.6 us (34%)
  blocking collectives  5.22 us (13%)
  Pallas kernels  2.87 us (7%)
  local copies, waits for them, and re-layouts  0.8 us (2%)
  between operations  0.67 us (2%)
    ppermute x1, waiting for transfers between devices, body(): lax.ppermute(mine, 'grp', [(i, i ^ groups // 2) for i in range(groups)])  12.6 us
    all_to_all x1, starting transfers between devices, body(): got = lax.all_to_all(payload, AXES, split_axis=0, concat_axis=0, tiled=True)  7.33 us
    all_gather x1, blocking collectives, body(): plane = lax.all_gather(both, 'seq', axis=0, axis_index_groups=neighbours)  5.22 us
    ppermute x3, waiting for transfers between devices, body(): pieces.append(lax.ppermute(plane, AXES, moves))  3.72 us
    ppermute x3, starting transfers between devices, body(): pieces.append(lax.ppermute(plane, AXES, moves))  3.49 us
    ppermute x1, starting transfers between devices, body(): lax.ppermute(mine, 'grp', [(i, i ^ groups // 2) for i in range(groups)])  2.74 us
    pallas_call x1, Pallas kernels, start(): pl.pallas_call(functools.partial(start_kernel, per_seq), out_shape=(jax.S...  1.99 us
    pallas_call x1, Pallas kernels, finish(): pl.pallas_call(functools.partial(finish_kernel, groups, shards, offsets,...  0.88 us
  transfers between devices with their start and end apart: 5, of which 4 were waited for; matrix products, arithmetic and copies ran while one was open for 0% of the time, Pallas kernels for 2%

profile of v3, /device:TPU:0, one launch (start us, length us, event | category | flops | bytes accessed | tf_op | source)
XLA Modules:
  0.0 39.4 jit_solution(10372854994231435152)
XLA Ops:
  0.6 2.0 %start.1 = (bf16[32,32,256]{2,1,0:T(8,128)(2,1)}, f32[16,128]{1,0:T(8,128)S(1)}) custom-call(s32[256]{0:T(256)} %dest_hbm.1, s32[8]{0:T(128)} %length_hbm.1, bf16[32,32,256]{2,1,0:T(8,128)(2,1)} %bitcast.11, bf16[4,128,256]{2,1,0:T(8,128)(2,1)} %key_hbm.1, bf16[4,128,256]{2,1,0:T(8,128)(2,1)} %value_hbm.1, bf16[8,64,128]{2,1,0:T(8,128)(2,1)} %query_hbm.1), custom_call_target="tpu_custom_call" | custom-call | tf_op jit(solution)/shard_map/start/pallas_call | solution.py:134
  2.6 7.3 %all-to-all-start = ((bf16[32,32,256]{2,1,0:T(8,128)(2,1)}), bf16[32,32,256]{2,1,0:T(8,128)(2,1)S(1)}, u32[]{:S(2)}, u32[]{:S(2)}) async-start(bf16[32,32,256]{2,1,0:T(8,128)(2,1)} %get-tuple-element.4), calls=%async_computation | async-start | bytes 1048576 | tf_op jit(solution)/shard_map/all_to_all | solution.py:219
  10.0 2.7 %collective-permute-start = (f32[16,128]{1,0:T(8,128)S(1)}, f32[16,128]{1,0:T(8,128)S(1)}, u32[]{:S(2)}, u32[]{:S(2)}) collective-permute-start(f32[16,128]{1,0:T(8,128)S(1)} %get-tuple-element.5), channel_id=1, source_target_pairs={{0,16},{8,24},{16,0},{24,8},{1,17},{9,25},{17,1},{25,9},{2,18},{10... | collective-permute-start | bytes 24584 | tf_op jit(solution)/shard_map/ppermute | solution.py:218
  12.7 12.6 %collective-permute-done = f32[16,128]{1,0:T(8,128)S(1)} collective-permute-done((f32[16,128]{1,0:T(8,128)S(1)}, f32[16,128]{1,0:T(8,128)S(1)}, u32[]{:S(2)}, u32[]{:S(2)}) %collective-permute-start) | collective-permute-done | bytes 8224 | tf_op jit(solution)/shard_map/ppermute | solution.py:218
  25.3 5.2 %all-gather = f32[8,16,128]{2,1,0:T(8,128)S(1)} all-gather(f32[2,16,128]{2,1,0:T(8,128)S(1)} %pad_maximum_fusion), channel_id=2, replica_groups={{0,1,2,3},{4,5,6,7},{8,9,10,11},{12,13,14,15},{16,17,18,19},{20,21,22,2..., dimensions={0}, use_global_device_ids=true | all-gather | bytes 81920 | tf_op jit(solution)/shard_map/all_gather | solution.py:222
  30.5 0.0 collective-permute-start.3
  30.5 2.9 %collective-permute-start.2 = (f32[4,2,16,128]{3,2,1,0:T(8,128)S(1)}, f32[4,2,16,128]{3,2,1,0:T(8,128)S(1)}, u32[]{:S(2)}, u32[]{:S(2)}) collective-permute-start(f32[4,2,16,128]{3,2,1,0:T(8,128)S(1)} %bitcast.6), channel_id=1, source_target_pairs={{8,0},{9,1},{10,2},{11,3},{12,4},{13,5},{14,6},{15,7},{0,8},{1,9},... | collective-permute-start | bytes 196616 | tf_op jit(solution)/shard_map/ppermute | solution.py:231
  33.5 0.5 %collective-permute-start.1 = (f32[4,2,16,128]{3,2,1,0:T(8,128)S(1)}, f32[4,2,16,128]{3,2,1,0:T(8,128)S(1)}, u32[]{:S(2)}, u32[]{:S(2)}) collective-permute-start(f32[4,2,16,128]{3,2,1,0:T(8,128)S(1)} %bitcast.7), channel_id=1, source_target_pairs={{4,0},{5,1},{6,2},{7,3},{0,4},{1,5},{2,6},{3,7},{12,8},{13,9},{14,... | collective-permute-start | bytes 196616 | tf_op jit(solution)/shard_map/ppermute | solution.py:231
  34.0 2.4 %collective-permute-done.3.refs_3_ = f32[4,2,16,128]{3,2,1,0:T(8,128)S(1)} collective-permute-done((f32[4,2,16,128]{3,2,1,0:T(8,128)S(1)}, f32[4,2,16,128]{3,2,1,0:T(8,128)S(1)}, u32[]{:S(2)}, u32[]{:S(2)}) %collective-permute-start.3) | collective-permute-done | bytes 65568 | tf_op jit(solution)/shard_map/ppermute | solution.py:231
  36.4 0.8 %collective-permute-done.2.refs_2_ = f32[4,2,16,128]{3,2,1,0:T(8,128)S(1)} collective-permute-done((f32[4,2,16,128]{3,2,1,0:T(8,128)S(1)}, f32[4,2,16,128]{3,2,1,0:T(8,128)S(1)}, u32[]{:S(2)}, u32[]{:S(2)}) %collective-permute-start.2) | collective-permute-done | bytes 65568 | tf_op jit(solution)/shard_map/ppermute | solution.py:231
  37.2 0.5 %collective-permute-done.1.refs_1_ = f32[4,2,16,128]{3,2,1,0:T(8,128)S(1)} collective-permute-done((f32[4,2,16,128]{3,2,1,0:T(8,128)S(1)}, f32[4,2,16,128]{3,2,1,0:T(8,128)S(1)}, u32[]{:S(2)}, u32[]{:S(2)}) %collective-permute-start.1) | collective-permute-done | bytes 65568 | tf_op jit(solution)/shard_map/ppermute | solution.py:231
  37.7 0.9 %finish.1 = f32[8,8192]{1,0:T(8,128)} custom-call(f32[4,2,16,128]{3,2,1,0:T(8,128)S(1)} %bitcast.8, f32[4,2,16,128]{3,2,1,0:T(8,128)S(1)} %collective-permute-done.1.refs_1_, f32[4,2,16,128]{3,2,1,0:T(8,128)S(1)} %collective-permute-done.2.refs_2_, f32[4,2,16,128]{3,2,1,0:T(8,128)S(1)} %collective-permute-done.3.refs_3_), custom_call_target="tpu_custom_call" | custom-call | tf_op jit(solution)/shard_map/finish/pallas_call | solution.py:195
  38.6 0.0 all-to-all-done
  38.6 0.8 %copy.9 = bf16[1,4,8,32,256]{4,3,2,1,0:T(8,128)(2,1)} copy(bf16[1,4,8,32,256]{4,3,2,1,0:T(8,128)(2,1)S(1)} %bitcast.10) | data formatting | bytes 1048576
  (1 shorter events, 0.0 us)
Async XLA Ops:
  2.6 36.0 %all-to-all-start = ((bf16[32,32,256]{2,1,0:T(8,128)(2,1)}), bf16[32,32,256]{2,1,0:T(8,128)(2,1)S(1)}, u32[]{:S(2)}, u32[]{:S(2)}) async-start(bf16[32,32,256]{2,1,0:T(8,128)(2,1)} %get-tuple-element.4), calls=%async_computation | async-start | bytes 1048576 | tf_op jit(solution)/shard_map/all_to_all | solution.py:219
  10.0 15.3 %collective-permute-start = (f32[16,128]{1,0:T(8,128)S(1)}, f32[16,128]{1,0:T(8,128)S(1)}, u32[]{:S(2)}, u32[]{:S(2)}) collective-permute-start(f32[16,128]{1,0:T(8,128)S(1)} %get-tuple-element.5), channel_id=1, source_target_pairs={{0,16},{8,24},{16,0},{24,8},{1,17},{9,25},{17,1},{25,9},{2,18},{10... | collective-permute-start | bytes 24584 | tf_op jit(solution)/shard_map/ppermute | solution.py:218
  30.5 5.9 %collective-permute-start.3 = (f32[4,2,16,128]{3,2,1,0:T(8,128)S(1)}, f32[4,2,16,128]{3,2,1,0:T(8,128)S(1)}, u32[]{:S(2)}, u32[]{:S(2)}) collective-permute-start(f32[4,2,16,128]{3,2,1,0:T(8,128)S(1)} %bitcast.5), channel_id=1, source_target_pairs={{12,0},{13,1},{14,2},{15,3},{8,4},{9,5},{10,6},{11,7},{4,8},{5,9},... | collective-permute-start | bytes 196616 | tf_op jit(solution)/shard_map/ppermute | solution.py:231
  30.5 6.7 %collective-permute-start.2 = (f32[4,2,16,128]{3,2,1,0:T(8,128)S(1)}, f32[4,2,16,128]{3,2,1,0:T(8,128)S(1)}, u32[]{:S(2)}, u32[]{:S(2)}) collective-permute-start(f32[4,2,16,128]{3,2,1,0:T(8,128)S(1)} %bitcast.6), channel_id=1, source_target_pairs={{8,0},{9,1},{10,2},{11,3},{12,4},{13,5},{14,6},{15,7},{0,8},{1,9},... | collective-permute-start | bytes 196616 | tf_op jit(solution)/shard_map/ppermute | solution.py:231
  33.5 4.3 %collective-permute-start.1 = (f32[4,2,16,128]{3,2,1,0:T(8,128)S(1)}, f32[4,2,16,128]{3,2,1,0:T(8,128)S(1)}, u32[]{:S(2)}, u32[]{:S(2)}) collective-permute-start(f32[4,2,16,128]{3,2,1,0:T(8,128)S(1)} %bitcast.7), channel_id=1, source_target_pairs={{4,0},{5,1},{6,2},{7,3},{0,4},{1,5},{2,6},{3,7},{12,8},{13,9},{14,... | collective-permute-start | bytes 196616 | tf_op jit(solution)/shard_map/ppermute | solution.py:231

commit v4 on v3

--- a/solution.py
+++ b/solution.py
@@ -153,19 +153,20 @@
     )(block_dest, lengths, latent, up_key, up_value, queries)
 
 
-def finish_kernel(groups, shards, offsets, heads, *refs):
-    sources, (result_hbm, result_ref, wide_ref, sem) = refs[: len(offsets)], refs[len(offsets) :]
+def finish_kernel(groups, shards, offsets, heads, got_ref, every_ref, blocks_hbm, result_hbm, result_ref, wide_ref, sems):
+    copy_blocks = pltpu.make_async_copy(got_ref, blocks_hbm, sems.at[0])
+    copy_blocks.start()
     batch = result_ref.shape[0]
     spans = shards // batch
-    near, halves, _, head_dim = sources[0].shape
+    near, halves = every_ref.shape[0], every_ref.shape[2]
     group = lax.axis_index("grp")
     major = lax.axis_index("seq") // near
-    for (step, flip), source in zip(offsets, sources):
+    for p, (step, flip) in enumerate(offsets):
         from_major = (major + step) % (shards // near)
         for half in range(halves):
             from_group = group ^ flip ^ (half * (groups // 2))
             for k in range(near):
-                wide_ref[from_group, from_major * near + k] = source[k, half]
+                wide_ref[from_group, from_major * near + k] = every_ref[k, p, half]
     if spans > 1:
         for g in range(groups):
             for b in range(batch):
@@ -178,32 +179,38 @@
                 accum = sum(x * f for x, f in zip(accums, factors))
                 total = sum(x * f for x, f in zip(totals, factors))
                 wide_ref[g, b, :heads] = accum / total
+    head_dim = every_ref.shape[4]
     for g in range(groups):
         for h in range(heads):
             column = (g * heads + h) * head_dim
             result_ref[:, column : column + head_dim] = wide_ref[g, :batch, h, :]
-    copy = pltpu.make_async_copy(result_ref, result_hbm, sem)
-    copy.start()
-    copy.wait()
-
-
-def finish(pieces, offsets, groups, shards, batch, heads):
-    rows, head_dim = pieces[0].shape[2:]
+    copy_result = pltpu.make_async_copy(result_ref, result_hbm, sems.at[1])
+    copy_result.start()
+    copy_blocks.wait()
+    copy_result.wait()
+
+
+def finish(got, every, offsets, groups, shards, batch, heads):
+    rows, head_dim = every.shape[3:]
     columns = groups * heads * head_dim
-    if in_vmem((len(pieces),) + pieces[0].shape):
-        pieces = [pltpu.with_memory_space_constraint(piece, pltpu.VMEM) for piece in pieces]
+    if in_vmem(every.shape) and in_vmem(got.shape):
+        got = pltpu.with_memory_space_constraint(got, pltpu.VMEM)
+        every = pltpu.with_memory_space_constraint(every, pltpu.VMEM)
     return pl.pallas_call(
         functools.partial(finish_kernel, groups, shards, offsets, heads),
-        out_shape=jax.ShapeDtypeStruct((batch, columns), F32),
-        in_specs=[pl.BlockSpec(memory_space=pltpu.VMEM)] * len(pieces),
-        out_specs=pl.BlockSpec(memory_space=pl.ANY),
+        out_shape=(
+            jax.ShapeDtypeStruct(got.shape, got.dtype),
+            jax.ShapeDtypeStruct((batch, columns), F32),
+        ),
+        in_specs=[pl.BlockSpec(memory_space=pltpu.VMEM)] * 2,
+        out_specs=(pl.BlockSpec(memory_space=pl.ANY),) * 2,
         scratch_shapes=[
             pltpu.VMEM((batch, columns), F32),
             pltpu.VMEM((groups, shards, rows, head_dim), F32),
-            pltpu.SemaphoreType.DMA,
+            pltpu.SemaphoreType.DMA((2,)),
         ],
         name="finish",
-    )(*pieces)
+    )(got, every)
 
 
 def body(latent, up_key, up_value, queries, lengths, block_dest):
@@ -218,19 +225,19 @@
     other = lax.ppermute(mine, "grp", [(i, i ^ (groups // 2)) for i in range(groups)])
     got = lax.all_to_all(payload, AXES, split_axis=0, concat_axis=0, tiled=True)
     both = jnp.stack([mine, other])
-    neighbours = [[k * near + i for i in range(near)] for k in range(far)]
-    plane = lax.all_gather(both, "seq", axis=0, axis_index_groups=neighbours)
     offsets = [(step, flip) for flip in range(groups // 2) for step in range(far)]
-    pieces = [plane]
+    pieces = [both]
     for step, flip in offsets[1:]:
         moves = [
             ((g ^ flip) * shards + (s + step * near) % shards, g * shards + s)
             for g in range(groups)
             for s in range(shards)
         ]
-        pieces.append(lax.ppermute(plane, AXES, moves))
-    attended = finish(pieces, offsets, groups, shards, batch, q_heads // groups)
-    return (got.reshape(1, groups, shards, block_len, width), attended)
+        pieces.append(lax.ppermute(both, AXES, moves))
+    neighbours = [[k * near + i for i in range(near)] for k in range(far)]
+    every = lax.all_gather(jnp.stack(pieces), "seq", axis=0, axis_index_groups=neighbours)
+    blocks, attended = finish(got, every, offsets, groups, shards, batch, q_heads // groups)
+    return (blocks.reshape(1, groups, shards, block_len, width), attended)
 
 
 def solution(mesh):

time: 39.7 us -> 38.3 us (0.965)
  waiting for transfers between devices: 16.3 us -> 15.2 us
  local copies, waits for them, and re-layouts: 0.8 us -> 0 us
  blocking collectives: 5.22 us -> 5.76 us
    ppermute x3, waiting for transfers between devices: 3.72 us -> 2.64 us  [body(): pieces.append(lax.ppermute(both, AXES, moves))]
    unnamed x1 -> x0, local copies, waits for them, and re-layouts: 0.8 us -> none
    all_gather x1, blocking collectives: 5.22 us -> 5.76 us  [body(): lax.all_gather(jnp.stack(pieces), 'seq', axis=0, axis_index_groups=neighb...]
  transfers between devices with their start and end apart: 5 -> 5, of which waited for: 4 -> 3; matrix products, arithmetic and copies ran while one was open for 0% -> 0% of each run, Pallas kernels for 2% -> 0%
where the time goes in v4:
time: 38.3 us; the launch traced here: 38.1 us
  waiting for transfers between devices  15.2 us (40%)
  starting transfers between devices  13.6 us (36%)
  blocking collectives  5.76 us (15%)
  Pallas kernels  2.88 us (8%)
  between operations  0.65 us (2%)
    ppermute x1, waiting for transfers between devices, body(): lax.ppermute(mine, 'grp', [(i, i ^ groups // 2) for i in range(groups)])  12.6 us
    all_to_all x1, starting transfers between devices, body(): got = lax.all_to_all(payload, AXES, split_axis=0, concat_axis=0, tiled=True)  7.33 us
    all_gather x1, blocking collectives, body(): lax.all_gather(jnp.stack(pieces), 'seq', axis=0, axis_index_groups=neighb...  5.76 us
    ppermute x3, starting transfers between devices, body(): pieces.append(lax.ppermute(both, AXES, moves))  3.49 us
    ppermute x1, starting transfers between devices, body(): lax.ppermute(mine, 'grp', [(i, i ^ groups // 2) for i in range(groups)])  2.74 us
    ppermute x3, waiting for transfers between devices, body(): pieces.append(lax.ppermute(both, AXES, moves))  2.64 us
    pallas_call x1, Pallas kernels, start(): pl.pallas_call(functools.partial(start_kernel, per_seq), out_shape=(jax.S...  1.99 us
    pallas_call x1, Pallas kernels, finish(): pl.pallas_call(functools.partial(finish_kernel, groups, shards, offsets,...  0.89 us
  transfers between devices with their start and end apart: 5, of which 3 were waited for; matrix products, arithmetic and copies ran while one was open for 0% of the time, Pallas kernels for 0%

profile of v4, /device:TPU:0, one launch (start us, length us, event | category | flops | bytes accessed | tf_op | source)
XLA Modules:
  0.0 38.1 jit_solution(1326851989771227427)
XLA Ops:
  0.6 2.0 %start.1 = (bf16[32,32,256]{2,1,0:T(8,128)(2,1)}, f32[16,128]{1,0:T(8,128)S(1)}) custom-call(s32[256]{0:T(256)} %dest_hbm.1, s32[8]{0:T(128)} %length_hbm.1, bf16[32,32,256]{2,1,0:T(8,128)(2,1)} %bitcast.12, bf16[4,128,256]{2,1,0:T(8,128)(2,1)} %key_hbm.1, bf16[4,128,256]{2,1,0:T(8,128)(2,1)} %value_hbm.1, bf16[8,64,128]{2,1,0:T(8,128)(2,1)} %query_hbm.1), custom_call_target="tpu_custom_call" | custom-call | tf_op jit(solution)/shard_map/start/pallas_call | solution.py:134
  2.6 7.3 %all-to-all-start = ((bf16[32,32,256]{2,1,0:T(8,128)(2,1)}), bf16[32,32,256]{2,1,0:T(8,128)(2,1)S(1)}, u32[]{:S(2)}, u32[]{:S(2)}) async-start(bf16[32,32,256]{2,1,0:T(8,128)(2,1)} %get-tuple-element.6), calls=%async_computation | async-start | bytes 1048576 | tf_op jit(solution)/shard_map/all_to_all | solution.py:226
  10.0 2.7 %collective-permute-start = (f32[16,128]{1,0:T(8,128)S(1)}, f32[16,128]{1,0:T(8,128)S(1)}, u32[]{:S(2)}, u32[]{:S(2)}) collective-permute-start(f32[16,128]{1,0:T(8,128)S(1)} %get-tuple-element.7), channel_id=1, source_target_pairs={{0,16},{8,24},{16,0},{24,8},{1,17},{9,25},{17,1},{25,9},{2,18},{10... | collective-permute-start | bytes 24584 | tf_op jit(solution)/shard_map/ppermute | solution.py:225
  12.7 12.6 %collective-permute-done = f32[16,128]{1,0:T(8,128)S(1)} collective-permute-done((f32[16,128]{1,0:T(8,128)S(1)}, f32[16,128]{1,0:T(8,128)S(1)}, u32[]{:S(2)}, u32[]{:S(2)}) %collective-permute-start) | collective-permute-done | bytes 8224 | tf_op jit(solution)/shard_map/ppermute | solution.py:225
  25.3 0.0 collective-permute-start.2
  25.3 1.5 %collective-permute-start.1 = (f32[2,16,128]{2,1,0:T(8,128)S(1)}, f32[2,16,128]{2,1,0:T(8,128)S(1)}, u32[]{:S(2)}, u32[]{:S(2)}) collective-permute-start(f32[2,16,128]{2,1,0:T(8,128)S(1)} %get-tuple-element.11), channel_id=1, source_target_pairs={{4,0},{5,1},{6,2},{7,3},{0,4},{1,5},{2,6},{3,7},{12,8},{13,9},{14,... | collective-permute-start | bytes 49160 | tf_op jit(solution)/shard_map/ppermute | solution.py:236
  26.8 2.0 %collective-permute-start.3 = (f32[2,16,128]{2,1,0:T(8,128)S(1)}, f32[2,16,128]{2,1,0:T(8,128)S(1)}, u32[]{:S(2)}, u32[]{:S(2)}) collective-permute-start(f32[2,16,128]{2,1,0:T(8,128)S(1)} %get-tuple-element.11), channel_id=1, source_target_pairs={{12,0},{13,1},{14,2},{15,3},{8,4},{9,5},{10,6},{11,7},{4,8},{5,9},... | collective-permute-start | bytes 49160 | tf_op jit(solution)/shard_map/ppermute | solution.py:236
  28.8 0.2 collective-permute-done.2
  29.0 0.0 collective-permute-done.1
  29.0 2.4 %collective-permute-done.3 = f32[2,16,128]{2,1,0:T(8,128)S(1)} collective-permute-done((f32[2,16,128]{2,1,0:T(8,128)S(1)}, f32[2,16,128]{2,1,0:T(8,128)S(1)}, u32[]{:S(2)}, u32[]{:S(2)}) %collective-permute-start.3) | collective-permute-done | bytes 16416 | tf_op jit(solution)/shard_map/ppermute | solution.py:236
  31.4 5.8 %all-gather = f32[16,2,16,128]{3,2,1,0:T(8,128)S(1)} all-gather(f32[4,2,16,128]{3,2,1,0:T(8,128)S(1)} %pad_maximum_fusion), channel_id=2, replica_groups={{0,1,2,3},{4,5,6,7},{8,9,10,11},{12,13,14,15},{16,17,18,19},{20,21,22,2..., dimensions={0}, use_global_device_ids=true | all-gather | bytes 327680 | tf_op jit(solution)/shard_map/all_gather | solution.py:238
  37.2 0.0 all-to-all-done.got_ref
  37.2 0.9 %finish.1 = (bf16[32,32,256]{2,1,0:T(8,128)(2,1)}, f32[8,8192]{1,0:T(8,128)}) custom-call(bf16[32,32,256]{2,1,0:T(8,128)(2,1)S(1)} %all-to-all-done.got_ref, f32[4,4,2,16,128]{4,3,2,1,0:T(8,128)S(1)} %bitcast.10), custom_call_target="tpu_custom_call" | custom-call | tf_op jit(solution)/shard_map/finish/pallas_call | solution.py:199
  (2 shorter events, 0.0 us)
Async XLA Ops:
  2.6 34.6 %all-to-all-start = ((bf16[32,32,256]{2,1,0:T(8,128)(2,1)}), bf16[32,32,256]{2,1,0:T(8,128)(2,1)S(1)}, u32[]{:S(2)}, u32[]{:S(2)}) async-start(bf16[32,32,256]{2,1,0:T(8,128)(2,1)} %get-tuple-element.6), calls=%async_computation | async-start | bytes 1048576 | tf_op jit(solution)/shard_map/all_to_all | solution.py:226
  10.0 15.3 %collective-permute-start = (f32[16,128]{1,0:T(8,128)S(1)}, f32[16,128]{1,0:T(8,128)S(1)}, u32[]{:S(2)}, u32[]{:S(2)}) collective-permute-start(f32[16,128]{1,0:T(8,128)S(1)} %get-tuple-element.7), channel_id=1, source_target_pairs={{0,16},{8,24},{16,0},{24,8},{1,17},{9,25},{17,1},{25,9},{2,18},{10... | collective-permute-start | bytes 24584 | tf_op jit(solution)/shard_map/ppermute | solution.py:225
  25.3 3.7 %collective-permute-start.2 = (f32[2,16,128]{2,1,0:T(8,128)S(1)}, f32[2,16,128]{2,1,0:T(8,128)S(1)}, u32[]{:S(2)}, u32[]{:S(2)}) collective-permute-start(f32[2,16,128]{2,1,0:T(8,128)S(1)} %get-tuple-element.11), channel_id=1, source_target_pairs={{8,0},{9,1},{10,2},{11,3},{12,4},{13,5},{14,6},{15,7},{0,8},{1,9},... | collective-permute-start | bytes 49160 | tf_op jit(solution)/shard_map/ppermute | solution.py:236
  25.3 3.7 %collective-permute-start.1 = (f32[2,16,128]{2,1,0:T(8,128)S(1)}, f32[2,16,128]{2,1,0:T(8,128)S(1)}, u32[]{:S(2)}, u32[]{:S(2)}) collective-permute-start(f32[2,16,128]{2,1,0:T(8,128)S(1)} %get-tuple-element.11), channel_id=1, source_target_pairs={{4,0},{5,1},{6,2},{7,3},{0,4},{1,5},{2,6},{3,7},{12,8},{13,9},{14,... | collective-permute-start | bytes 49160 | tf_op jit(solution)/shard_map/ppermute | solution.py:236
  26.8 4.6 %collective-permute-start.3 = (f32[2,16,128]{2,1,0:T(8,128)S(1)}, f32[2,16,128]{2,1,0:T(8,128)S(1)}, u32[]{:S(2)}, u32[]{:S(2)}) collective-permute-start(f32[2,16,128]{2,1,0:T(8,128)S(1)} %get-tuple-element.11), channel_id=1, source_target_pairs={{12,0},{13,1},{14,2},{15,3},{8,4},{9,5},{10,6},{11,7},{4,8},{5,9},... | collective-permute-start | bytes 49160 | tf_op jit(solution)/shard_map/ppermute | solution.py:236

commit v5 on v4

--- a/solution.py
+++ b/solution.py
@@ -153,20 +153,24 @@
     )(block_dest, lengths, latent, up_key, up_value, queries)
 
 
-def finish_kernel(groups, shards, offsets, heads, got_ref, every_ref, blocks_hbm, result_hbm, result_ref, wide_ref, sems):
+def finish_kernel(groups, shards, offsets, heads, got_ref, *refs):
+    pieces, (blocks_hbm, result_hbm, result_ref, wide_ref, sems) = (
+        refs[: len(offsets)],
+        refs[len(offsets) :],
+    )
     copy_blocks = pltpu.make_async_copy(got_ref, blocks_hbm, sems.at[0])
     copy_blocks.start()
     batch = result_ref.shape[0]
     spans = shards // batch
-    near, halves = every_ref.shape[0], every_ref.shape[2]
+    near, halves, _, head_dim = pieces[0].shape
     group = lax.axis_index("grp")
     major = lax.axis_index("seq") // near
-    for p, (step, flip) in enumerate(offsets):
+    for (step, flip), piece in zip(offsets, pieces):
         from_major = (major + step) % (shards // near)
         for half in range(halves):
             from_group = group ^ flip ^ (half * (groups // 2))
             for k in range(near):
-                wide_ref[from_group, from_major * near + k] = every_ref[k, p, half]
+                wide_ref[from_group, from_major * near + k] = piece[k, half]
     if spans > 1:
         for g in range(groups):
             for b in range(batch):
@@ -179,7 +183,6 @@
                 accum = sum(x * f for x, f in zip(accums, factors))
                 total = sum(x * f for x, f in zip(totals, factors))
                 wide_ref[g, b, :heads] = accum / total
-    head_dim = every_ref.shape[4]
     for g in range(groups):
         for h in range(heads):
             column = (g * heads + h) * head_dim
@@ -190,19 +193,19 @@
     copy_result.wait()
 
 
-def finish(got, every, offsets, groups, shards, batch, heads):
-    rows, head_dim = every.shape[3:]
+def finish(got, pieces, offsets, groups, shards, batch, heads):
+    rows, head_dim = pieces[0].shape[2:]
     columns = groups * heads * head_dim
-    if in_vmem(every.shape) and in_vmem(got.shape):
+    if in_vmem(got.shape):
         got = pltpu.with_memory_space_constraint(got, pltpu.VMEM)
-        every = pltpu.with_memory_space_constraint(every, pltpu.VMEM)
+        pieces = [pltpu.with_memory_space_constraint(piece, pltpu.VMEM) for piece in pieces]
     return pl.pallas_call(
         functools.partial(finish_kernel, groups, shards, offsets, heads),
         out_shape=(
             jax.ShapeDtypeStruct(got.shape, got.dtype),
             jax.ShapeDtypeStruct((batch, columns), F32),
         ),
-        in_specs=[pl.BlockSpec(memory_space=pltpu.VMEM)] * 2,
+        in_specs=[pl.BlockSpec(memory_space=pltpu.VMEM)] * (1 + len(pieces)),
         out_specs=(pl.BlockSpec(memory_space=pl.ANY),) * 2,
         scratch_shapes=[
             pltpu.VMEM((batch, columns), F32),
@@ -210,7 +213,7 @@
             pltpu.SemaphoreType.DMA((2,)),
         ],
         name="finish",
-    )(got, every)
+    )(got, *pieces)
 
 
 def body(latent, up_key, up_value, queries, lengths, block_dest):
@@ -225,18 +228,18 @@
     other = lax.ppermute(mine, "grp", [(i, i ^ (groups // 2)) for i in range(groups)])
     got = lax.all_to_all(payload, AXES, split_axis=0, concat_axis=0, tiled=True)
     both = jnp.stack([mine, other])
+    neighbours = [[k * near + i for i in range(near)] for k in range(far)]
+    plane = lax.all_gather(both, "seq", axis=0, axis_index_groups=neighbours)
     offsets = [(step, flip) for flip in range(groups // 2) for step in range(far)]
-    pieces = [both]
+    pieces = [plane]
     for step, flip in offsets[1:]:
         moves = [
             ((g ^ flip) * shards + (s + step * near) % shards, g * shards + s)
             for g in range(groups)
             for s in range(shards)
         ]
-        pieces.append(lax.ppermute(both, AXES, moves))
-    neighbours = [[k * near + i for i in range(near)] for k in range(far)]
-    every = lax.all_gather(jnp.stack(pieces), "seq", axis=0, axis_index_groups=neighbours)
-    blocks, attended = finish(got, every, offsets, groups, shards, batch, q_heads // groups)
+        pieces.append(lax.ppermute(plane, AXES, moves))
+    blocks, attended = finish(got, pieces, offsets, groups, shards, batch, q_heads // groups)
     return (blocks.reshape(1, groups, shards, block_len, width), attended)
 
 

time: 38.3 us -> 38.9 us (1.016)
  waiting for transfers between devices: 15.2 us -> 16.3 us
  blocking collectives: 5.76 us -> 5.22 us
    ppermute x3, waiting for transfers between devices: 2.64 us -> 3.72 us  [body(): pieces.append(lax.ppermute(plane, AXES, moves))]
    all_gather x1, blocking collectives: 5.76 us -> 5.22 us  [body(): plane = lax.all_gather(both, 'seq', axis=0, axis_index_groups=neighbours)]
  transfers between devices with their start and end apart: 5 -> 5, of which waited for: 3 -> 4; matrix products, arithmetic and copies ran while one was open for 0% -> 0% of each run, Pallas kernels for 0% -> 0%
where the time goes in v5:
time: 38.9 us; the launch traced here: 38.6 us
  waiting for transfers between devices  16.3 us (42%)
  starting transfers between devices  13.6 us (35%)
  blocking collectives  5.22 us (13%)
  Pallas kernels  2.88 us (7%)
  between operations  0.65 us (2%)
    ppermute x1, waiting for transfers between devices, body(): lax.ppermute(mine, 'grp', [(i, i ^ groups // 2) for i in range(groups)])  12.6 us
    all_to_all x1, starting transfers between devices, body(): got = lax.all_to_all(payload, AXES, split_axis=0, concat_axis=0, tiled=True)  7.33 us
    all_gather x1, blocking collectives, body(): plane = lax.all_gather(both, 'seq', axis=0, axis_index_groups=neighbours)  5.22 us
    ppermute x3, waiting for transfers between devices, body(): pieces.append(lax.ppermute(plane, AXES, moves))  3.72 us
    ppermute x3, starting transfers between devices, body(): pieces.append(lax.ppermute(plane, AXES, moves))  3.49 us
    ppermute x1, starting transfers between devices, body(): lax.ppermute(mine, 'grp', [(i, i ^ groups // 2) for i in range(groups)])  2.74 us
    pallas_call x1, Pallas kernels, start(): pl.pallas_call(functools.partial(start_kernel, per_seq), out_shape=(jax.S...  1.99 us
    pallas_call x1, Pallas kernels, finish(): pl.pallas_call(functools.partial(finish_kernel, groups, shards, offsets,...  0.89 us
  transfers between devices with their start and end apart: 5, of which 4 were waited for; matrix products, arithmetic and copies ran while one was open for 0% of the time, Pallas kernels for 0%

profile of v5, /device:TPU:0, one launch (start us, length us, event | category | flops | bytes accessed | tf_op | source)
XLA Modules:
  0.0 38.6 jit_solution(3520918801776775808)
XLA Ops:
  0.6 2.0 %start.1 = (bf16[32,32,256]{2,1,0:T(8,128)(2,1)}, f32[16,128]{1,0:T(8,128)S(1)}) custom-call(s32[256]{0:T(256)} %dest_hbm.1, s32[8]{0:T(128)} %length_hbm.1, bf16[32,32,256]{2,1,0:T(8,128)(2,1)} %bitcast.10, bf16[4,128,256]{2,1,0:T(8,128)(2,1)} %key_hbm.1, bf16[4,128,256]{2,1,0:T(8,128)(2,1)} %value_hbm.1, bf16[8,64,128]{2,1,0:T(8,128)(2,1)} %query_hbm.1), custom_call_target="tpu_custom_call" | custom-call | tf_op jit(solution)/shard_map/start/pallas_call | solution.py:134
  2.6 7.3 %all-to-all-start = ((bf16[32,32,256]{2,1,0:T(8,128)(2,1)}), bf16[32,32,256]{2,1,0:T(8,128)(2,1)S(1)}, u32[]{:S(2)}, u32[]{:S(2)}) async-start(bf16[32,32,256]{2,1,0:T(8,128)(2,1)} %get-tuple-element.6), calls=%async_computation | async-start | bytes 1048576 | tf_op jit(solution)/shard_map/all_to_all | solution.py:229
  10.0 2.7 %collective-permute-start = (f32[16,128]{1,0:T(8,128)S(1)}, f32[16,128]{1,0:T(8,128)S(1)}, u32[]{:S(2)}, u32[]{:S(2)}) collective-permute-start(f32[16,128]{1,0:T(8,128)S(1)} %get-tuple-element.7), channel_id=1, source_target_pairs={{0,16},{8,24},{16,0},{24,8},{1,17},{9,25},{17,1},{25,9},{2,18},{10... | collective-permute-start | bytes 24584 | tf_op jit(solution)/shard_map/ppermute | solution.py:228
  12.7 12.6 %collective-permute-done = f32[16,128]{1,0:T(8,128)S(1)} collective-permute-done((f32[16,128]{1,0:T(8,128)S(1)}, f32[16,128]{1,0:T(8,128)S(1)}, u32[]{:S(2)}, u32[]{:S(2)}) %collective-permute-start) | collective-permute-done | bytes 8224 | tf_op jit(solution)/shard_map/ppermute | solution.py:228
  25.3 5.2 %all-gather = f32[8,16,128]{2,1,0:T(8,128)S(1)} all-gather(f32[2,16,128]{2,1,0:T(8,128)S(1)} %pad_maximum_fusion), channel_id=2, replica_groups={{0,1,2,3},{4,5,6,7},{8,9,10,11},{12,13,14,15},{16,17,18,19},{20,21,22,2..., dimensions={0}, use_global_device_ids=true | all-gather | bytes 81920 | tf_op jit(solution)/shard_map/all_gather | solution.py:232
  30.5 0.0 collective-permute-start.3
  30.5 2.9 %collective-permute-start.2 = (f32[4,2,16,128]{3,2,1,0:T(8,128)S(1)}, f32[4,2,16,128]{3,2,1,0:T(8,128)S(1)}, u32[]{:S(2)}, u32[]{:S(2)}) collective-permute-start(f32[4,2,16,128]{3,2,1,0:T(8,128)S(1)} %bitcast.6), channel_id=1, source_target_pairs={{8,0},{9,1},{10,2},{11,3},{12,4},{13,5},{14,6},{15,7},{0,8},{1,9},... | collective-permute-start | bytes 196616 | tf_op jit(solution)/shard_map/ppermute | solution.py:241
  33.5 0.5 %collective-permute-start.1 = (f32[4,2,16,128]{3,2,1,0:T(8,128)S(1)}, f32[4,2,16,128]{3,2,1,0:T(8,128)S(1)}, u32[]{:S(2)}, u32[]{:S(2)}) collective-permute-start(f32[4,2,16,128]{3,2,1,0:T(8,128)S(1)} %bitcast.7), channel_id=1, source_target_pairs={{4,0},{5,1},{6,2},{7,3},{0,4},{1,5},{2,6},{3,7},{12,8},{13,9},{14,... | collective-permute-start | bytes 196616 | tf_op jit(solution)/shard_map/ppermute | solution.py:241
  34.0 2.4 %collective-permute-done.3.refs_3_ = f32[4,2,16,128]{3,2,1,0:T(8,128)S(1)} collective-permute-done((f32[4,2,16,128]{3,2,1,0:T(8,128)S(1)}, f32[4,2,16,128]{3,2,1,0:T(8,128)S(1)}, u32[]{:S(2)}, u32[]{:S(2)}) %collective-permute-start.3) | collective-permute-done | bytes 65568 | tf_op jit(solution)/shard_map/ppermute | solution.py:241
  36.4 0.8 %collective-permute-done.2.refs_2_ = f32[4,2,16,128]{3,2,1,0:T(8,128)S(1)} collective-permute-done((f32[4,2,16,128]{3,2,1,0:T(8,128)S(1)}, f32[4,2,16,128]{3,2,1,0:T(8,128)S(1)}, u32[]{:S(2)}, u32[]{:S(2)}) %collective-permute-start.2) | collective-permute-done | bytes 65568 | tf_op jit(solution)/shard_map/ppermute | solution.py:241
  37.2 0.5 %collective-permute-done.1.refs_1_ = f32[4,2,16,128]{3,2,1,0:T(8,128)S(1)} collective-permute-done((f32[4,2,16,128]{3,2,1,0:T(8,128)S(1)}, f32[4,2,16,128]{3,2,1,0:T(8,128)S(1)}, u32[]{:S(2)}, u32[]{:S(2)}) %collective-permute-start.1) | collective-permute-done | bytes 65568 | tf_op jit(solution)/shard_map/ppermute | solution.py:241
  37.7 0.0 all-to-all-done.got_ref
  37.7 0.9 %finish.1 = (bf16[32,32,256]{2,1,0:T(8,128)(2,1)}, f32[8,8192]{1,0:T(8,128)}) custom-call(bf16[32,32,256]{2,1,0:T(8,128)(2,1)S(1)} %all-to-all-done.got_ref, f32[4,2,16,128]{3,2,1,0:T(8,128)S(1)} %bitcast.8, f32[4,2,16,128]{3,2,1,0:T(8,128)S(1)} %collective-permute-done.1.refs_1_, f32[4,2,16,128]{3,2,1,0:T(8,128)S(1)} %collective-permute-done.2.refs_2_, ...), custom_call_target="tpu_custom_call" | custom-call | tf_op jit(solution)/shard_map/finish/pallas_call | solution.py:202
  (1 shorter events, 0.0 us)
Async XLA Ops:
  2.6 35.1 %all-to-all-start = ((bf16[32,32,256]{2,1,0:T(8,128)(2,1)}), bf16[32,32,256]{2,1,0:T(8,128)(2,1)S(1)}, u32[]{:S(2)}, u32[]{:S(2)}) async-start(bf16[32,32,256]{2,1,0:T(8,128)(2,1)} %get-tuple-element.6), calls=%async_computation | async-start | bytes 1048576 | tf_op jit(solution)/shard_map/all_to_all | solution.py:229
  10.0 15.3 %collective-permute-start = (f32[16,128]{1,0:T(8,128)S(1)}, f32[16,128]{1,0:T(8,128)S(1)}, u32[]{:S(2)}, u32[]{:S(2)}) collective-permute-start(f32[16,128]{1,0:T(8,128)S(1)} %get-tuple-element.7), channel_id=1, source_target_pairs={{0,16},{8,24},{16,0},{24,8},{1,17},{9,25},{17,1},{25,9},{2,18},{10... | collective-permute-start | bytes 24584 | tf_op jit(solution)/shard_map/ppermute | solution.py:228
  30.5 5.9 %collective-permute-start.3 = (f32[4,2,16,128]{3,2,1,0:T(8,128)S(1)}, f32[4,2,16,128]{3,2,1,0:T(8,128)S(1)}, u32[]{:S(2)}, u32[]{:S(2)}) collective-permute-start(f32[4,2,16,128]{3,2,1,0:T(8,128)S(1)} %bitcast.5), channel_id=1, source_target_pairs={{12,0},{13,1},{14,2},{15,3},{8,4},{9,5},{10,6},{11,7},{4,8},{5,9},... | collective-permute-start | bytes 196616 | tf_op jit(solution)/shard_map/ppermute | solution.py:241
  30.5 6.7 %collective-permute-start.2 = (f32[4,2,16,128]{3,2,1,0:T(8,128)S(1)}, f32[4,2,16,128]{3,2,1,0:T(8,128)S(1)}, u32[]{:S(2)}, u32[]{:S(2)}) collective-permute-start(f32[4,2,16,128]{3,2,1,0:T(8,128)S(1)} %bitcast.6), channel_id=1, source_target_pairs={{8,0},{9,1},{10,2},{11,3},{12,4},{13,5},{14,6},{15,7},{0,8},{1,9},... | collective-permute-start | bytes 196616 | tf_op jit(solution)/shard_map/ppermute | solution.py:241
  33.5 4.3 %collective-permute-start.1 = (f32[4,2,16,128]{3,2,1,0:T(8,128)S(1)}, f32[4,2,16,128]{3,2,1,0:T(8,128)S(1)}, u32[]{:S(2)}, u32[]{:S(2)}) collective-permute-start(f32[4,2,16,128]{3,2,1,0:T(8,128)S(1)} %bitcast.7), channel_id=1, source_target_pairs={{4,0},{5,1},{6,2},{7,3},{0,4},{1,5},{2,6},{3,7},{12,8},{13,9},{14,... | collective-permute-start | bytes 196616 | tf_op jit(solution)/shard_map/ppermute | solution.py:241

commit v6 on v4

v6 whole, which is shorter than its diff:
```python
import functools
import math

import jax
import jax.numpy as jnp
from jax import lax
from jax.experimental import pallas as pl
from jax.experimental.pallas import tpu as pltpu
from jax.sharding import PartitionSpec as P


AXES = ("grp", "seq")
F32 = jnp.float32
BF16 = jnp.bfloat16
NEAR_BYTES = 1 << 20
TAIL = 8
LANES = 128


def parts_of(x, count):
    parts = []
    for _ in range(count):
        part = x.astype(BF16)
        parts.append(part)
        x = x - part.astype(F32)
    return parts


def exact_dot(x, y, contract):
    rows = x.shape[0]
    wide = lax.dot_general(
        jnp.concatenate(parts_of(x, 3), axis=0),
        y,
        (contract, ((), ())),
        preferred_element_type=F32,
    )
    return wide[:rows] + (wide[rows : 2 * rows] + wide[2 * rows :])


def in_vmem(*arrays):
    if sum(math.prod(x.shape) * x.dtype.itemsize for x in arrays) > NEAR_BYTES:
        return arrays
    return tuple(pltpu.with_memory_space_constraint(x, pltpu.VMEM) for x in arrays)


def start_kernel(
    per_seq,
    sent,
    groups,
    shards,
    dest_hbm,
    length_hbm,
    lat_hbm,
    key_hbm,
    value_hbm,
    query_hbm,
    out_hbm,
    side_0,
    side_1,
    dest,
    length,
    lat_ref,
    key_ref,
    value_ref,
    query_ref,
    ordered_ref,
    tails_ref,
    sems,
):
    slots, block_len, width = lat_ref.shape
    kept = ordered_ref.shape[1]
    rank = width // 2
    heads, head_dim = query_ref.shape
    per_group = key_ref.shape[1] // head_dim
    per_kv = heads // per_group
    scale = 1.0 / float(head_dim) ** 0.5
    group = lax.axis_index("grp")
    shard = lax.axis_index("seq")
    first = shard * slots
    seq = first // per_seq
    begin = (first % per_seq) * block_len
    rows = pl.ds(pl.multiple_of(group * heads, heads), heads)
    sources = (lat_hbm, dest_hbm, key_hbm.at[group], query_hbm.at[seq, rows], length_hbm, value_hbm.at[group])
    targets = (lat_ref, dest, key_ref, query_ref, length, value_ref)
    copies = [
        pltpu.make_async_copy(source, target, sems.at[k])
        for k, (source, target) in enumerate(zip(sources, targets))
    ]
    for copy in copies:
        copy.start()
    for copy in copies:
        copy.wait()

    def move(j, carry):
        target = dest[first + j]
        for c in range(width // LANES):
            lanes = slice(c * LANES, (c + 1) * LANES)
            height = min(block_len, kept - c * block_len)
            ordered_ref[target, c * block_len : c * block_len + height, :] = lat_ref[j, :height, lanes]
        tails_ref[target] = lat_ref[j, block_len - TAIL :, width - LANES :]
        return carry

    lax.fori_loop(0, slots, move, 0, unroll=8)
    send = pltpu.make_async_copy(ordered_ref, out_hbm, sems.at[len(copies)])
    send.start()

    far = shards // 2
    half = groups // 2
    count = half * far
    sides = (side_0, side_1)
    for over in range(2):
        for core in range(2):
            for flip in range(half):
                for step in range(far):
                    target = ((group ^ flip) ^ (over * half)) * shards + (
                        (shard // 2 + step) % far * 2 + core
                    )
                    sides[over][core * count + flip * far + step] = tails_ref[target]

    tokens = slots * block_len
    lat = lat_ref[...].reshape(tokens, width)
    absorbed = []
    for k in range(per_group):
        columns = slice(k * head_dim, (k + 1) * head_dim)
        absorbed.append(
            lax.dot_general(
                query_ref[k * per_kv : (k + 1) * per_kv, :],
                key_ref[:, columns],
                (((1,), (1,)), ((), ())),
                preferred_element_type=F32,
            )
        )
    absorbed = jnp.concatenate(absorbed, axis=0)
    scores = exact_dot(absorbed, lat[:, :rank], ((1,), (1,))) * scale
    position = begin + lax.broadcasted_iota(jnp.int32, scores.shape, 1)
    live = position < length[seq]
    scores = jnp.where(live, scores, -1e30)
    top = jnp.max(scores, axis=1, keepdims=True)
    weights = jnp.where(live, jnp.exp(scores - top), 0.0)
    total = jnp.sum(weights, axis=1, keepdims=True)
    mixed = exact_dot(weights, lat[:, rank:], ((1,), (0,)))
    if per_seq == slots:
        mixed = mixed / total
    attended = []
    for k in range(per_group):
        columns = slice(k * head_dim, (k + 1) * head_dim)
        attended.append(
            exact_dot(mixed[k * per_kv : (k + 1) * per_kv], value_ref[:, columns], ((1,), (0,)))
        )
    fields = list(attended)
    if per_seq != slots:
        for field in (top, total):
            for k in range(per_group):
                fields.append(
                    jnp.broadcast_to(field[k * per_kv : (k + 1) * per_kv], (per_kv, head_dim))
                )
    parts = [part for field in fields for part in parts_of(field, sent)]
    for side in sides:
        for p, part in enumerate(parts):
            side[2 * count + p] = part
    send.wait()


def start(latent, up_key, up_value, queries, lengths, block_dest, groups, shards, sent, fields):
    _, block_len, width = latent.shape
    batch, q_heads, head_dim = queries.shape
    heads = q_heads // groups
    per_seq = block_dest.shape[0] // batch
    kept = block_len * (width // LANES) - TAIL
    dests = groups * shards
    side = (groups // 2 * shards + sent * fields, TAIL, LANES)
    vmem = pl.BlockSpec(memory_space=pltpu.VMEM)
    return pl.pallas_call(
        functools.partial(start_kernel, per_seq, sent, groups, shards),
        out_shape=(jax.ShapeDtypeStruct((dests, kept, LANES), latent.dtype),)
        + (pltpu.VMEM(side, latent.dtype),) * 2,
        in_specs=[pl.BlockSpec(memory_space=pl.ANY)] * 6,
        out_specs=(pl.BlockSpec(memory_space=pl.ANY),) + (vmem,) * 2,
        scratch_shapes=[
            pltpu.SMEM(block_dest.shape, jnp.int32),
            pltpu.SMEM(lengths.shape, jnp.int32),
            pltpu.VMEM(latent.shape, latent.dtype),
            pltpu.VMEM(up_key.shape[1:], up_key.dtype),
            pltpu.VMEM(up_value.shape[1:], up_value.dtype),
            pltpu.VMEM((heads, head_dim), queries.dtype),
            pltpu.VMEM((dests, kept, LANES), latent.dtype),
            pltpu.VMEM((dests, TAIL, LANES), latent.dtype),
            pltpu.SemaphoreType.DMA((7,)),
        ],
        name="start",
    )(block_dest, lengths, latent, up_key, up_value, queries)


def pack_kernel(pair_ref, *parcels):
    count = len(parcels)
    tiles = pair_ref.shape[2]
    core = lax.axis_index("seq") % 2
    for k, parcel in enumerate(parcels):
        for over in range(2):
            for source in range(2):
                q = over * 2 + source
                parcel[q, 0] = pair_ref[source, over, core * count + k]
                for p in range(tiles - 2 * count):
                    parcel[q, 1 + p] = pair_ref[source, over, 2 * count + p]


def pack(pair, count):
    tiles, tail, width = pair.shape[2:]
    parcel = (4, 1 + tiles - 2 * count, tail, width)
    (pair,) = in_vmem(pair)
    vmem = pl.BlockSpec(memory_space=pltpu.VMEM)
    small = 2 * count * math.prod(parcel) <= NEAR_BYTES
    shape = (pltpu.VMEM if small else jax.ShapeDtypeStruct)(parcel, pair.dtype)
    return pl.pallas_call(
        pack_kernel,
        out_shape=(shape,) * count,
        in_specs=[vmem],
        out_specs=(vmem,) * count,
        name="pack",
    )(pair)


def finish_kernel(groups, shards, offsets, sent, got_ref, *refs):
    count = len(offsets)
    parcels, (blocks_hbm, result_hbm, result_ref, wide_ref, tails_ref, sems) = refs[:count], refs[count:]
    kept = got_ref.shape[1]
    block_len, width = blocks_hbm.shape[1:]
    copies = []
    for c in range(width // LANES):
        height = min(block_len, kept - c * block_len)
        copies.append(
            pltpu.make_async_copy(
                got_ref.at[:, pl.ds(c * block_len, height), :],
                blocks_hbm.at[:, pl.ds(0, height), pl.ds(c * LANES, LANES)],
                sems.at[c],
            )
        )
        copies[-1].start()
    batch, _ = result_ref.shape
    spans = shards // batch
    far, half = shards // 2, groups // 2
    fields, per_group = wide_ref.shape[2:4]
    group = lax.axis_index("grp")
    shard = lax.axis_index("seq")
    for (flip, step), parcel in zip(offsets, parcels):
        for q in range(4):
            source_group = (group ^ flip) ^ (q // 2 * half)
            source_shard = (shard // 2 - step + far) % far * 2 + q % 2
            tails_ref[source_group * shards + source_shard] = parcel[q, 0]
            for f in range(fields):
                for k in range(per_group):
                    first = 1 + (f * per_group + k) * sent
                    wide_ref[source_group, source_shard, f, k] = sum(
                        parcel[q, first + p].astype(F32) for p in reversed(range(sent))
                    )
    copies.append(
        pltpu.make_async_copy(
            tails_ref,
            blocks_hbm.at[:, pl.ds(block_len - TAIL, TAIL), pl.ds(width - LANES, LANES)],
            sems.at[width // LANES],
        )
    )
    copies[-1].start()
    if spans > 1:
        for g in range(groups):
            for b in range(batch):
                pieces = [wide_ref[g, b * spans + k] for k in range(spans)]
                top = functools.reduce(jnp.maximum, [piece[1] for piece in pieces])
                factors = [jnp.exp(piece[1] - top) for piece in pieces]
                accum = sum(piece[0] * f for piece, f in zip(pieces, factors))
                total = sum(piece[2] * f for piece, f in zip(pieces, factors))
                wide_ref[g, b, 0] = accum / total
    for g in range(groups):
        for k in range(per_group):
            for j in range(TAIL):
                column = ((g * per_group + k) * TAIL + j) * LANES
                result_ref[:, column : column + LANES] = wide_ref[g, :batch, 0, k, j, :]
    copies.append(pltpu.make_async_copy(result_ref, result_hbm, sems.at[width // LANES + 1]))
    copies[-1].start()
    for copy in copies:
        copy.wait()


def finish(got, parcels, offsets, groups, shards, batch, block_len, width, per_group, sent):
    dests = got.shape[0]
    fields = (parcels[0].shape[1] - 1) // (sent * per_group)
    columns = groups * per_group * TAIL * LANES
    got, *parcels = in_vmem(got, *parcels)
    return pl.pallas_call(
        functools.partial(finish_kernel, groups, shards, offsets, sent),
        out_shape=(
            jax.ShapeDtypeStruct((dests, block_len, width), got.dtype),
            jax.ShapeDtypeStruct((batch, columns), F32),
        ),
        in_specs=[pl.BlockSpec(memory_space=pltpu.VMEM)] * (1 + len(parcels)),
        out_specs=(pl.BlockSpec(memory_space=pl.ANY),) * 2,
        scratch_shapes=[
            pltpu.VMEM((batch, columns), F32),
            pltpu.VMEM((groups, shards, fields, per_group, TAIL, LANES), F32),
            pltpu.VMEM((dests, TAIL, LANES), got.dtype),
            pltpu.SemaphoreType.DMA((width // LANES + 2,)),
        ],
        name="finish",
    )(got, *parcels)


def sending_order(half, far):
    even, odd = list(range(0, far, 2)), list(range(1, far, 2))
    order = [(flip, step) for flip in range(half - 1, 0, -1) for step in odd + even[::-1]]
    return order + [(0, step) for step in even[1:] + odd]


def body(latent, up_key, up_value, queries, lengths, block_dest):
    groups = up_key.shape[0]
    _, block_len, width = latent.shape[1:]
    batch, q_heads, head_dim = queries.shape
    shards = lax.axis_size("seq")
    far, half = shards // 2, groups // 2
    assert groups == 2 * half and shards == 2 * far and shards % batch == 0
    per_group = up_key.shape[2] // head_dim
    assert head_dim == LANES and q_heads == groups * per_group * TAIL
    sent, fields = (2, 1) if shards == batch else (3, 3)
    payload, mine, other = start(
        latent[0], up_key, up_value, queries, lengths, block_dest, groups, shards, sent, fields * per_group
    )
    devices = [(g, s) for g in range(groups) for s in range(shards)]
    other = lax.ppermute(other, "grp", [(g, g ^ half) for g in range(groups)])
    got = lax.all_to_all(payload, AXES, split_axis=0, concat_axis=0, tiled=True)
    cores = [[2 * k, 2 * k + 1] for k in range(far)]
    pair = lax.all_gather(jnp.stack([mine, other]), "seq", axis=0, axis_index_groups=cores)
    offsets = [(flip, step) for flip in range(half) for step in range(far)]
    parcels = list(pack(pair, len(offsets)))
    for flip, step in sending_order(half, far):
        k = offsets.index((flip, step))
        moves = [(g * shards + s, (g ^ flip) * shards + (s + 2 * step) % shards) for g, s in devices]
        parcels[k] = lax.ppermute(parcels[k], AXES, moves)
    blocks, attended = finish(
        got, parcels, offsets, groups, shards, batch, block_len, width, per_group, sent
    )
    return (blocks.reshape(1, groups, shards, block_len, width), attended)


def solution(mesh):
    return jax.shard_map(
        body,
        mesh=mesh,
        in_specs=(P("grp", "seq", None, None), P(), P(), P(), P(), P()),
        out_specs=(P(AXES, None, None, None, None), P()),
        check_vma=False,
    )
```

time: 38.3 us -> 41.3 us (1.078)
  starting transfers between devices: 13.6 us -> 20.4 us
  blocking collectives: 5.76 us -> 1.92 us
    ppermute x4 -> x8, starting transfers between devices: 6.23 us -> 13 us  [the longest x7 10.3 us: body(): parcels[k] = lax.ppermute(parcels[k], AXES, moves)]
    all_gather x1, blocking collectives: 5.76 us -> 1.92 us  [body(): lax.all_gather(jnp.stack([mine, other]), 'seq', axis=0, axis_index_groups...]
    ppermute x4 -> x8, waiting for transfers between devices: 15.2 us -> 15 us  [the longest x1 12.6 us: body(): other = lax.ppermute(other, 'grp', [(g, g ^ half) for g in range(groups)])]
    pallas_call x1 -> x2, Pallas kernels: 1.99 us -> 2.09 us  [the longest x1 2.05 us: start(): pl.pallas_call(functools.partial(start_kernel, per_seq, sent, groups, sha...]
  transfers between devices with their start and end apart: 5 -> 9, of which waited for: 3 -> 4; matrix products, arithmetic and copies ran while one was open for 0% -> 0% of each run, Pallas kernels for 0% -> 0%
where the time goes in v6:
time: 41.3 us; the launch traced here: 41 us
  starting transfers between devices  20.4 us (49%)
  waiting for transfers between devices  15 us (36%)
  Pallas kernels  3.02 us (7%)
  blocking collectives  1.92 us (5%)
  between operations  0.67 us (2%)
    ppermute x1, waiting for transfers between devices, body(): other = lax.ppermute(other, 'grp', [(g, g ^ half) for g in range(groups)])  12.6 us
    ppermute x7, starting transfers between devices, body(): parcels[k] = lax.ppermute(parcels[k], AXES, moves)  10.3 us
    all_to_all x1, starting transfers between devices, body(): got = lax.all_to_all(payload, AXES, split_axis=0, concat_axis=0, tiled=True)  7.33 us
    ppermute x1, starting transfers between devices, body(): other = lax.ppermute(other, 'grp', [(g, g ^ half) for g in range(groups)])  2.74 us
    ppermute x7, waiting for transfers between devices, body(): parcels[k] = lax.ppermute(parcels[k], AXES, moves)  2.44 us
    pallas_call x1, Pallas kernels, start(): pl.pallas_call(functools.partial(start_kernel, per_seq, sent, groups, sha...  2.05 us
    all_gather x1, blocking collectives, body(): lax.all_gather(jnp.stack([mine, other]), 'seq', axis=0, axis_index_groups...  1.92 us
    pallas_call x1, Pallas kernels, finish(): pl.pallas_call(functools.partial(finish_kernel, groups, shards, offsets,...  0.93 us
  transfers between devices with their start and end apart: 9, of which 4 were waited for; matrix products, arithmetic and copies ran while one was open for 0% of the time, Pallas kernels for 0%

profile of v6, /device:TPU:0, one launch (start us, length us, event | category | flops | bytes accessed | tf_op | source)
XLA Modules:
  0.0 41.0 jit_solution(3570468457298570148)
XLA Ops:
  0.6 2.0 %start.1 = (bf16[32,56,128]{2,1,0:T(8,128)(2,1)}, bf16[20,8,128]{2,1,0:T(8,128)(2,1)S(1)}, bf16[20,8,128]{2,1,0:T(8,128)(2,1)S(1)}) custom-call(s32[256]{0:T(256)} %dest_hbm.1, s32[8]{0:T(128)} %length_hbm.1, bf16[32,32,256]{2,1,0:T(8,128)(2,1)} %bitcast.7, bf16[4,128,256]{2,1,0:T(8,128)(2,1)} %key_hbm.1, bf16[4,128,256]{2,1,0:T(8,128)(2,1)} %value_hbm.1, ...), custom_call_target="tpu_custom_call" | custom-call | tf_op jit(solution)/shard_map/start/pallas_call | solution.py:173
  2.7 7.3 %all-to-all-start = ((bf16[32,56,128]{2,1,0:T(8,128)(2,1)}), bf16[32,56,128]{2,1,0:T(8,128)(2,1)S(1)}, u32[]{:S(2)}, u32[]{:S(2)}) async-start(bf16[32,56,128]{2,1,0:T(8,128)(2,1)} %get-tuple-element.15), calls=%async_computation | async-start | bytes 917504 | tf_op jit(solution)/shard_map/all_to_all | solution.py:328
  10.0 2.7 %collective-permute-start = (bf16[20,8,128]{2,1,0:T(8,128)(2,1)S(1)}, bf16[20,8,128]{2,1,0:T(8,128)(2,1)S(1)}, u32[]{:S(2)}, u32[]{:S(2)}) collective-permute-start(bf16[20,8,128]{2,1,0:T(8,128)(2,1)S(1)} %get-tuple-element.17), channel_id=1, source_target_pairs={{0,16},{8,24},{16,0},{24,8},{1,17},{9,25},{17,1},{25,9},{2,18},{10... | collective-permute-start | bytes 122888 | tf_op jit(solution)/shard_map/ppermute | solution.py:327
  12.8 12.6 %collective-permute-done = bf16[20,8,128]{2,1,0:T(8,128)(2,1)S(1)} collective-permute-done((bf16[20,8,128]{2,1,0:T(8,128)(2,1)S(1)}, bf16[20,8,128]{2,1,0:T(8,128)(2,1)S(1)}, u32[]{:S(2)}, u32[]{:S(2)}) %collective-permute-start) | collective-permute-done | bytes 40992 | tf_op jit(solution)/shard_map/ppermute | solution.py:327
  25.4 1.9 %all-gather = bf16[4,20,8,128]{3,2,1,0:T(8,128)(2,1)S(1)} all-gather(bf16[2,20,8,128]{3,2,1,0:T(8,128)(2,1)S(1)} %pad_maximum_fusion), channel_id=2, replica_groups={{0,1},{2,3},{4,5},{6,7},{8,9},{10,11},{12,13},{14,15},{16,17},{18,19},{..., dimensions={0}, use_global_device_ids=true | all-gather | bytes 245760 | tf_op jit(solution)/shard_map/all_gather | solution.py:330
  27.3 1.5 %collective-permute-start.1 = (bf16[4,5,8,128]{3,2,1,0:T(8,128)(2,1)S(1)}, bf16[4,5,8,128]{3,2,1,0:T(8,128)(2,1)S(1)}, u32[]{:S(2)}, u32[]{:S(2)}) collective-permute-start(bf16[4,5,8,128]{3,2,1,0:T(8,128)(2,1)S(1)} %get-tuple-element.19), channel_id=1, source_target_pairs={{0,2},{1,3},{2,4},{3,5},{4,6},{5,7},{6,0},{7,1},{8,10},{9,11},{10,... | collective-permute-start | bytes 122888 | tf_op jit(solution)/shard_map/ppermute | solution.py:336
  28.9 1.5 %collective-permute-start.2 = (bf16[4,5,8,128]{3,2,1,0:T(8,128)(2,1)S(1)}, bf16[4,5,8,128]{3,2,1,0:T(8,128)(2,1)S(1)}, u32[]{:S(2)}, u32[]{:S(2)}) collective-permute-start(bf16[4,5,8,128]{3,2,1,0:T(8,128)(2,1)S(1)} %get-tuple-element.20), channel_id=1, source_target_pairs={{0,4},{1,5},{2,6},{3,7},{4,0},{5,1},{6,2},{7,3},{8,12},{9,13},{10,... | collective-permute-start | bytes 122888 | tf_op jit(solution)/shard_map/ppermute | solution.py:336
  30.3 1.4 %collective-permute-start.3 = (bf16[4,5,8,128]{3,2,1,0:T(8,128)(2,1)S(1)}, bf16[4,5,8,128]{3,2,1,0:T(8,128)(2,1)S(1)}, u32[]{:S(2)}, u32[]{:S(2)}) collective-permute-start(bf16[4,5,8,128]{3,2,1,0:T(8,128)(2,1)S(1)} %get-tuple-element.21), channel_id=1, source_target_pairs={{0,6},{1,7},{2,0},{3,1},{4,2},{5,3},{6,4},{7,5},{8,14},{9,15},{10,... | collective-permute-start | bytes 122888 | tf_op jit(solution)/shard_map/ppermute | solution.py:336
  31.8 0.0 collective-permute-start.4
  31.8 2.0 %collective-permute-start.5 = (bf16[4,5,8,128]{3,2,1,0:T(8,128)(2,1)S(1)}, bf16[4,5,8,128]{3,2,1,0:T(8,128)(2,1)S(1)}, u32[]{:S(2)}, u32[]{:S(2)}) collective-permute-start(bf16[4,5,8,128]{3,2,1,0:T(8,128)(2,1)S(1)} %get-tuple-element.23), channel_id=1, source_target_pairs={{0,10},{1,11},{2,12},{3,13},{4,14},{5,15},{6,8},{7,9},{8,2},{9,3},... | collective-permute-start | bytes 122888 | tf_op jit(solution)/shard_map/ppermute | solution.py:336
  33.8 0.0 collective-permute-done.1.refs_1_
  33.8 0.0 collective-permute-start.6
  33.8 0.0 collective-permute-done.2.refs_2_
  33.8 3.8 %collective-permute-start.7 = (bf16[4,5,8,128]{3,2,1,0:T(8,128)(2,1)S(1)}, bf16[4,5,8,128]{3,2,1,0:T(8,128)(2,1)S(1)}, u32[]{:S(2)}, u32[]{:S(2)}) collective-permute-start(bf16[4,5,8,128]{3,2,1,0:T(8,128)(2,1)S(1)} %get-tuple-element.25), channel_id=1, source_target_pairs={{0,14},{1,15},{2,8},{3,9},{4,10},{5,11},{6,12},{7,13},{8,6},{9,7},... | collective-permute-start | bytes 122888 | tf_op jit(solution)/shard_map/ppermute | solution.py:336
  37.6 0.0 collective-permute-done.3.refs_3_
  37.6 0.0 collective-permute-done.4.refs_4_
  37.6 0.4 collective-permute-done.5.refs_5_
  38.0 0.7 %collective-permute-done.6.refs_6_ = bf16[4,5,8,128]{3,2,1,0:T(8,128)(2,1)S(1)} collective-permute-done((bf16[4,5,8,128]{3,2,1,0:T(8,128)(2,1)S(1)}, bf16[4,5,8,128]{3,2,1,0:T(8,128)(2,1)S(1)}, u32[]{:S(2)}, u32[]{:S(2)}) %collective-permute-start.6) | collective-permute-done | bytes 40992 | tf_op jit(solution)/shard_map/ppermute | solution.py:336
  38.8 1.3 %collective-permute-done.7.refs_7_ = bf16[4,5,8,128]{3,2,1,0:T(8,128)(2,1)S(1)} collective-permute-done((bf16[4,5,8,128]{3,2,1,0:T(8,128)(2,1)S(1)}, bf16[4,5,8,128]{3,2,1,0:T(8,128)(2,1)S(1)}, u32[]{:S(2)}, u32[]{:S(2)}) %collective-permute-start.7) | collective-permute-done | bytes 40992 | tf_op jit(solution)/shard_map/ppermute | solution.py:336
  40.1 0.0 all-to-all-done.got_ref
  40.1 0.9 %finish.1 = (bf16[32,32,256]{2,1,0:T(8,128)(2,1)}, f32[8,8192]{1,0:T(8,128)}) custom-call(bf16[32,56,128]{2,1,0:T(8,128)(2,1)S(1)} %all-to-all-done.got_ref, bf16[4,5,8,128]{3,2,1,0:T(8,128)(2,1)S(1)} %get-tuple-element.18.refs_0_, bf16[4,5,8,128]{3,2,1,0:T(8,128)(2,1)S(1)} %collective-permute-done.1.refs_1_, ...), custom_call_target="tpu_custom_call" | custom-call | tf_op jit(solution)/shard_map/finish/pallas_call | solution.py:289
  (2 shorter events, 0.1 us)
Async XLA Ops:
  2.7 37.4 %all-to-all-start = ((bf16[32,56,128]{2,1,0:T(8,128)(2,1)}), bf16[32,56,128]{2,1,0:T(8,128)(2,1)S(1)}, u32[]{:S(2)}, u32[]{:S(2)}) async-start(bf16[32,56,128]{2,1,0:T(8,128)(2,1)} %get-tuple-element.15), calls=%async_computation | async-start | bytes 917504 | tf_op jit(solution)/shard_map/all_to_all | solution.py:328
  10.0 15.3 %collective-permute-start = (bf16[20,8,128]{2,1,0:T(8,128)(2,1)S(1)}, bf16[20,8,128]{2,1,0:T(8,128)(2,1)S(1)}, u32[]{:S(2)}, u32[]{:S(2)}) collective-permute-start(bf16[20,8,128]{2,1,0:T(8,128)(2,1)S(1)} %get-tuple-element.17), channel_id=1, source_target_pairs={{0,16},{8,24},{16,0},{24,8},{1,17},{9,25},{17,1},{25,9},{2,18},{10... | collective-permute-start | bytes 122888 | tf_op jit(solution)/shard_map/ppermute | solution.py:327
  27.3 6.5 %collective-permute-start.1 = (bf16[4,5,8,128]{3,2,1,0:T(8,128)(2,1)S(1)}, bf16[4,5,8,128]{3,2,1,0:T(8,128)(2,1)S(1)}, u32[]{:S(2)}, u32[]{:S(2)}) collective-permute-start(bf16[4,5,8,128]{3,2,1,0:T(8,128)(2,1)S(1)} %get-tuple-element.19), channel_id=1, source_target_pairs={{0,2},{1,3},{2,4},{3,5},{4,6},{5,7},{6,0},{7,1},{8,10},{9,11},{10,... | collective-permute-start | bytes 122888 | tf_op jit(solution)/shard_map/ppermute | solution.py:336
  28.9 5.0 %collective-permute-start.2 = (bf16[4,5,8,128]{3,2,1,0:T(8,128)(2,1)S(1)}, bf16[4,5,8,128]{3,2,1,0:T(8,128)(2,1)S(1)}, u32[]{:S(2)}, u32[]{:S(2)}) collective-permute-start(bf16[4,5,8,128]{3,2,1,0:T(8,128)(2,1)S(1)} %get-tuple-element.20), channel_id=1, source_target_pairs={{0,4},{1,5},{2,6},{3,7},{4,0},{5,1},{6,2},{7,3},{8,12},{9,13},{10,... | collective-permute-start | bytes 122888 | tf_op jit(solution)/shard_map/ppermute | solution.py:336
  30.3 7.3 %collective-permute-start.3 = (bf16[4,5,8,128]{3,2,1,0:T(8,128)(2,1)S(1)}, bf16[4,5,8,128]{3,2,1,0:T(8,128)(2,1)S(1)}, u32[]{:S(2)}, u32[]{:S(2)}) collective-permute-start(bf16[4,5,8,128]{3,2,1,0:T(8,128)(2,1)S(1)} %get-tuple-element.21), channel_id=1, source_target_pairs={{0,6},{1,7},{2,0},{3,1},{4,2},{5,3},{6,4},{7,5},{8,14},{9,15},{10,... | collective-permute-start | bytes 122888 | tf_op jit(solution)/shard_map/ppermute | solution.py:336
  31.8 5.8 %collective-permute-start.4 = (bf16[4,5,8,128]{3,2,1,0:T(8,128)(2,1)S(1)}, bf16[4,5,8,128]{3,2,1,0:T(8,128)(2,1)S(1)}, u32[]{:S(2)}, u32[]{:S(2)}) collective-permute-start(bf16[4,5,8,128]{3,2,1,0:T(8,128)(2,1)S(1)} %get-tuple-element.22), channel_id=1, source_target_pairs={{0,8},{1,9},{2,10},{3,11},{4,12},{5,13},{6,14},{7,15},{8,0},{9,1},... | collective-permute-start | bytes 122888 | tf_op jit(solution)/shard_map/ppermute | solution.py:336
  31.8 6.2 %collective-permute-start.5 = (bf16[4,5,8,128]{3,2,1,0:T(8,128)(2,1)S(1)}, bf16[4,5,8,128]{3,2,1,0:T(8,128)(2,1)S(1)}, u32[]{:S(2)}, u32[]{:S(2)}) collective-permute-start(bf16[4,5,8,128]{3,2,1,0:T(8,128)(2,1)S(1)} %get-tuple-element.23), channel_id=1, source_target_pairs={{0,10},{1,11},{2,12},{3,13},{4,14},{5,15},{6,8},{7,9},{8,2},{9,3},... | collective-permute-start | bytes 122888 | tf_op jit(solution)/shard_map/ppermute | solution.py:336
  33.8 4.9 %collective-permute-start.6 = (bf16[4,5,8,128]{3,2,1,0:T(8,128)(2,1)S(1)}, bf16[4,5,8,128]{3,2,1,0:T(8,128)(2,1)S(1)}, u32[]{:S(2)}, u32[]{:S(2)}) collective-permute-start(bf16[4,5,8,128]{3,2,1,0:T(8,128)(2,1)S(1)} %get-tuple-element.24), channel_id=1, source_target_pairs={{0,12},{1,13},{2,14},{3,15},{4,8},{5,9},{6,10},{7,11},{8,4},{9,5},... | collective-permute-start | bytes 122888 | tf_op jit(solution)/shard_map/ppermute | solution.py:336
  33.8 6.2 %collective-permute-start.7 = (bf16[4,5,8,128]{3,2,1,0:T(8,128)(2,1)S(1)}, bf16[4,5,8,128]{3,2,1,0:T(8,128)(2,1)S(1)}, u32[]{:S(2)}, u32[]{:S(2)}) collective-permute-start(bf16[4,5,8,128]{3,2,1,0:T(8,128)(2,1)S(1)} %get-tuple-element.25), channel_id=1, source_target_pairs={{0,14},{1,15},{2,8},{3,9},{4,10},{5,11},{6,12},{7,13},{8,6},{9,7},... | collective-permute-start | bytes 122888 | tf_op jit(solution)/shard_map/ppermute | solution.py:336

commit v7 on v6

--- a/solution.py
+++ b/solution.py
@@ -100,7 +100,7 @@
         tails_ref[target] = lat_ref[j, block_len - TAIL :, width - LANES :]
         return carry
 
-    lax.fori_loop(0, slots, move, 0, unroll=8)
+    lax.fori_loop(0, slots, move, 0, unroll=min(slots, 32))
     send = pltpu.make_async_copy(ordered_ref, out_hbm, sems.at[len(copies)])
     send.start()
 
@@ -191,33 +191,33 @@
     )(block_dest, lengths, latent, up_key, up_value, queries)
 
 
-def pack_kernel(pair_ref, *parcels):
+def pack_kernel(mine_ref, other_ref, *parcels):
     count = len(parcels)
-    tiles = pair_ref.shape[2]
+    tiles = mine_ref.shape[1]
     core = lax.axis_index("seq") % 2
     for k, parcel in enumerate(parcels):
         for over in range(2):
-            for source in range(2):
-                q = over * 2 + source
-                parcel[q, 0] = pair_ref[source, over, core * count + k]
+            for swap, pair_ref in enumerate((mine_ref, other_ref)):
+                q = over * 2 + swap
+                parcel[q, 0] = pair_ref[over, core * count + k]
                 for p in range(tiles - 2 * count):
-                    parcel[q, 1 + p] = pair_ref[source, over, 2 * count + p]
-
-
-def pack(pair, count):
-    tiles, tail, width = pair.shape[2:]
+                    parcel[q, 1 + p] = pair_ref[over, 2 * count + p]
+
+
+def pack(mine, other, count):
+    tiles, tail, width = mine.shape[1:]
     parcel = (4, 1 + tiles - 2 * count, tail, width)
-    (pair,) = in_vmem(pair)
+    mine, other = in_vmem(mine, other)
     vmem = pl.BlockSpec(memory_space=pltpu.VMEM)
     small = 2 * count * math.prod(parcel) <= NEAR_BYTES
-    shape = (pltpu.VMEM if small else jax.ShapeDtypeStruct)(parcel, pair.dtype)
+    shape = (pltpu.VMEM if small else jax.ShapeDtypeStruct)(parcel, mine.dtype)
     return pl.pallas_call(
         pack_kernel,
         out_shape=(shape,) * count,
-        in_specs=[vmem],
+        in_specs=[vmem] * 2,
         out_specs=(vmem,) * count,
         name="pack",
-    )(pair)
+    )(mine, other)
 
 
 def finish_kernel(groups, shards, offsets, sent, got_ref, *refs):
@@ -245,7 +245,7 @@
     for (flip, step), parcel in zip(offsets, parcels):
         for q in range(4):
             source_group = (group ^ flip) ^ (q // 2 * half)
-            source_shard = (shard // 2 - step + far) % far * 2 + q % 2
+            source_shard = (shard // 2 - step + far) % far * 2 + (shard + q) % 2
             tails_ref[source_group * shards + source_shard] = parcel[q, 0]
             for f in range(fields):
                 for k in range(per_group):
@@ -305,9 +305,13 @@
 
 
 def sending_order(half, far):
-    even, odd = list(range(0, far, 2)), list(range(1, far, 2))
-    order = [(flip, step) for flip in range(half - 1, 0, -1) for step in odd + even[::-1]]
-    return order + [(0, step) for step in even[1:] + odd]
+    steps = list(range(1, far, 2)) + list(range(0, far, 2))[::-1]
+    across = [(flip, step) for flip in range(half - 1, 0, -1) for step in steps]
+    within = [(0, step) for step in range(1, far)]
+    order = []
+    for n in range(0, max(len(across), len(within)), 2):
+        order += across[n : n + 2] + within[n : n + 2]
+    return order
 
 
 def body(latent, up_key, up_value, queries, lengths, block_dest):
@@ -326,10 +330,10 @@
     devices = [(g, s) for g in range(groups) for s in range(shards)]
     other = lax.ppermute(other, "grp", [(g, g ^ half) for g in range(groups)])
     got = lax.all_to_all(payload, AXES, split_axis=0, concat_axis=0, tiled=True)
-    cores = [[2 * k, 2 * k + 1] for k in range(far)]
-    pair = lax.all_gather(jnp.stack([mine, other]), "seq", axis=0, axis_index_groups=cores)
+    pair = jnp.stack([mine, other])
+    beside = lax.ppermute(pair, "seq", [(s, s ^ 1) for s in range(shards)])
     offsets = [(flip, step) for flip in range(half) for step in range(far)]
-    parcels = list(pack(pair, len(offsets)))
+    parcels = list(pack(pair, beside, len(offsets)))
     for flip, step in sending_order(half, far):
         k = offsets.index((flip, step))
         moves = [(g * shards + s, (g ^ flip) * shards + (s + 2 * step) % shards) for g, s in devices]

time: 41.3 us -> 41.2 us (level)
  blocking collectives: 1.92 us -> 0 us
  waiting for transfers between devices: 15 us -> 16.3 us
  Pallas kernels: 3.02 us -> 3.56 us
    all_gather x1 -> x0, blocking collectives: 1.92 us -> none  [body(): lax.all_gather(jnp.stack([mine, other]), 'seq', axis=0, axis_index_groups...]
    ppermute x0 -> x1, waiting for transfers between devices: none -> 1.26 us  [body(): beside = lax.ppermute(pair, 'seq', [(s, s ^ 1) for s in range(shards)])]
    pallas_call x1, Pallas kernels: 2.05 us -> 2.54 us  [start(): pl.pallas_call(functools.partial(start_kernel, per_seq, sent, groups, sha...]
  transfers between devices with their start and end apart: 9 -> 10, of which waited for: 4 -> 5; matrix products, arithmetic and copies ran while one was open for 0% -> 0% of each run, Pallas kernels for 0% -> 0%
where the time goes in v7:
time: 41.2 us; the launch traced here: 41 us
  starting transfers between devices  20.4 us (50%)
  waiting for transfers between devices  16.3 us (40%)
  Pallas kernels  3.56 us (9%)
  between operations  0.67 us (2%)
    ppermute x1, waiting for transfers between devices, body(): other = lax.ppermute(other, 'grp', [(g, g ^ half) for g in range(groups)])  12.6 us
    ppermute x7, starting transfers between devices, body(): parcels[k] = lax.ppermute(parcels[k], AXES, moves)  10.3 us
    all_to_all x1, starting transfers between devices, body(): got = lax.all_to_all(payload, AXES, split_axis=0, concat_axis=0, tiled=True)  7.33 us
    ppermute x1, starting transfers between devices, body(): other = lax.ppermute(other, 'grp', [(g, g ^ half) for g in range(groups)])  2.74 us
    pallas_call x1, Pallas kernels, start(): pl.pallas_call(functools.partial(start_kernel, per_seq, sent, groups, sha...  2.54 us
    ppermute x7, waiting for transfers between devices, body(): parcels[k] = lax.ppermute(parcels[k], AXES, moves)  2.44 us
    ppermute x1, waiting for transfers between devices, body(): beside = lax.ppermute(pair, 'seq', [(s, s ^ 1) for s in range(shards)])  1.26 us
    pallas_call x1, Pallas kernels, finish(): pl.pallas_call(functools.partial(finish_kernel, groups, shards, offsets,...  0.98 us
  transfers between devices with their start and end apart: 10, of which 5 were waited for; matrix products, arithmetic and copies ran while one was open for 0% of the time, Pallas kernels for 0%

profile of v7, /device:TPU:0, one launch (start us, length us, event | category | flops | bytes accessed | tf_op | source)
XLA Modules:
  0.0 41.0 jit_solution(3535435201833499056)
XLA Ops:
  0.6 2.5 %start.1 = (bf16[32,56,128]{2,1,0:T(8,128)(2,1)}, bf16[20,8,128]{2,1,0:T(8,128)(2,1)S(1)}, bf16[20,8,128]{2,1,0:T(8,128)(2,1)S(1)}) custom-call(s32[256]{0:T(256)} %dest_hbm.1, s32[8]{0:T(128)} %length_hbm.1, bf16[32,32,256]{2,1,0:T(8,128)(2,1)} %bitcast.5, bf16[4,128,256]{2,1,0:T(8,128)(2,1)} %key_hbm.1, bf16[4,128,256]{2,1,0:T(8,128)(2,1)} %value_hbm.1, ...), custom_call_target="tpu_custom_call" | custom-call | tf_op jit(solution)/shard_map/start/pallas_call | solution.py:173
  3.2 7.3 %all-to-all-start = ((bf16[32,56,128]{2,1,0:T(8,128)(2,1)}), bf16[32,56,128]{2,1,0:T(8,128)(2,1)S(1)}, u32[]{:S(2)}, u32[]{:S(2)}) async-start(bf16[32,56,128]{2,1,0:T(8,128)(2,1)} %get-tuple-element.15), calls=%async_computation | async-start | bytes 917504 | tf_op jit(solution)/shard_map/all_to_all | solution.py:332
  10.5 2.7 %collective-permute-start = (bf16[20,8,128]{2,1,0:T(8,128)(2,1)S(1)}, bf16[20,8,128]{2,1,0:T(8,128)(2,1)S(1)}, u32[]{:S(2)}, u32[]{:S(2)}) collective-permute-start(bf16[20,8,128]{2,1,0:T(8,128)(2,1)S(1)} %get-tuple-element.17), channel_id=1, source_target_pairs={{0,16},{8,24},{16,0},{24,8},{1,17},{9,25},{17,1},{25,9},{2,18},{10... | collective-permute-start | bytes 122888 | tf_op jit(solution)/shard_map/ppermute | solution.py:331
  13.3 12.6 %collective-permute-done = bf16[20,8,128]{2,1,0:T(8,128)(2,1)S(1)} collective-permute-done((bf16[20,8,128]{2,1,0:T(8,128)(2,1)S(1)}, bf16[20,8,128]{2,1,0:T(8,128)(2,1)S(1)}, u32[]{:S(2)}, u32[]{:S(2)}) %collective-permute-start) | collective-permute-done | bytes 40992 | tf_op jit(solution)/shard_map/ppermute | solution.py:331
  25.8 0.1 collective-permute-start.1
  25.9 1.3 %collective-permute-done.1.other_ref = bf16[2,20,8,128]{3,2,1,0:T(8,128)(2,1)S(1)} collective-permute-done((bf16[2,20,8,128]{3,2,1,0:T(8,128)(2,1)S(1)}, bf16[2,20,8,128]{3,2,1,0:T(8,128)(2,1)S(1)}, u32[]{:S(2)}, u32[]{:S(2)}) %collective-permute-start.1) | collective-permute-done | bytes 81952 | tf_op jit(solution)/shard_map/ppermute | solution.py:334
  27.2 1.5 %collective-permute-start.2 = (bf16[4,5,8,128]{3,2,1,0:T(8,128)(2,1)S(1)}, bf16[4,5,8,128]{3,2,1,0:T(8,128)(2,1)S(1)}, u32[]{:S(2)}, u32[]{:S(2)}) collective-permute-start(bf16[4,5,8,128]{3,2,1,0:T(8,128)(2,1)S(1)} %get-tuple-element.19), channel_id=1, source_target_pairs={{0,2},{1,3},{2,4},{3,5},{4,6},{5,7},{6,0},{7,1},{8,10},{9,11},{10,... | collective-permute-start | bytes 122888 | tf_op jit(solution)/shard_map/ppermute | solution.py:340
  28.8 1.5 %collective-permute-start.3 = (bf16[4,5,8,128]{3,2,1,0:T(8,128)(2,1)S(1)}, bf16[4,5,8,128]{3,2,1,0:T(8,128)(2,1)S(1)}, u32[]{:S(2)}, u32[]{:S(2)}) collective-permute-start(bf16[4,5,8,128]{3,2,1,0:T(8,128)(2,1)S(1)} %get-tuple-element.20), channel_id=1, source_target_pairs={{0,4},{1,5},{2,6},{3,7},{4,0},{5,1},{6,2},{7,3},{8,12},{9,13},{10,... | collective-permute-start | bytes 122888 | tf_op jit(solution)/shard_map/ppermute | solution.py:340
  30.3 1.4 %collective-permute-start.4 = (bf16[4,5,8,128]{3,2,1,0:T(8,128)(2,1)S(1)}, bf16[4,5,8,128]{3,2,1,0:T(8,128)(2,1)S(1)}, u32[]{:S(2)}, u32[]{:S(2)}) collective-permute-start(bf16[4,5,8,128]{3,2,1,0:T(8,128)(2,1)S(1)} %get-tuple-element.21), channel_id=1, source_target_pairs={{0,6},{1,7},{2,0},{3,1},{4,2},{5,3},{6,4},{7,5},{8,14},{9,15},{10,... | collective-permute-start | bytes 122888 | tf_op jit(solution)/shard_map/ppermute | solution.py:340
  31.7 0.0 collective-permute-start.5
  31.7 2.0 %collective-permute-start.6 = (bf16[4,5,8,128]{3,2,1,0:T(8,128)(2,1)S(1)}, bf16[4,5,8,128]{3,2,1,0:T(8,128)(2,1)S(1)}, u32[]{:S(2)}, u32[]{:S(2)}) collective-permute-start(bf16[4,5,8,128]{3,2,1,0:T(8,128)(2,1)S(1)} %get-tuple-element.23), channel_id=1, source_target_pairs={{0,10},{1,11},{2,12},{3,13},{4,14},{5,15},{6,8},{7,9},{8,2},{9,3},... | collective-permute-start | bytes 122888 | tf_op jit(solution)/shard_map/ppermute | solution.py:340
  33.7 0.0 collective-permute-done.2.refs_1_
  33.7 0.0 collective-permute-start.7
  33.8 0.0 collective-permute-done.3.refs_2_
  33.8 3.8 %collective-permute-start.8 = (bf16[4,5,8,128]{3,2,1,0:T(8,128)(2,1)S(1)}, bf16[4,5,8,128]{3,2,1,0:T(8,128)(2,1)S(1)}, u32[]{:S(2)}, u32[]{:S(2)}) collective-permute-start(bf16[4,5,8,128]{3,2,1,0:T(8,128)(2,1)S(1)} %get-tuple-element.25), channel_id=1, source_target_pairs={{0,14},{1,15},{2,8},{3,9},{4,10},{5,11},{6,12},{7,13},{8,6},{9,7},... | collective-permute-start | bytes 122888 | tf_op jit(solution)/shard_map/ppermute | solution.py:340
  37.5 0.0 collective-permute-done.4.refs_3_
  37.5 0.0 collective-permute-done.5.refs_4_
  37.5 0.4 collective-permute-done.6.refs_5_
  37.9 0.7 %collective-permute-done.7.refs_6_ = bf16[4,5,8,128]{3,2,1,0:T(8,128)(2,1)S(1)} collective-permute-done((bf16[4,5,8,128]{3,2,1,0:T(8,128)(2,1)S(1)}, bf16[4,5,8,128]{3,2,1,0:T(8,128)(2,1)S(1)}, u32[]{:S(2)}, u32[]{:S(2)}) %collective-permute-start.7) | collective-permute-done | bytes 40992 | tf_op jit(solution)/shard_map/ppermute | solution.py:340
  38.7 1.3 %collective-permute-done.8.refs_7_ = bf16[4,5,8,128]{3,2,1,0:T(8,128)(2,1)S(1)} collective-permute-done((bf16[4,5,8,128]{3,2,1,0:T(8,128)(2,1)S(1)}, bf16[4,5,8,128]{3,2,1,0:T(8,128)(2,1)S(1)}, u32[]{:S(2)}, u32[]{:S(2)}) %collective-permute-start.8) | collective-permute-done | bytes 40992 | tf_op jit(solution)/shard_map/ppermute | solution.py:340
  40.0 0.0 all-to-all-done.got_ref
  40.0 1.0 %finish.1 = (bf16[32,32,256]{2,1,0:T(8,128)(2,1)}, f32[8,8192]{1,0:T(8,128)}) custom-call(bf16[32,56,128]{2,1,0:T(8,128)(2,1)S(1)} %all-to-all-done.got_ref, bf16[4,5,8,128]{3,2,1,0:T(8,128)(2,1)S(1)} %get-tuple-element.18.refs_0_, bf16[4,5,8,128]{3,2,1,0:T(8,128)(2,1)S(1)} %collective-permute-done.2.refs_1_, ...), custom_call_target="tpu_custom_call" | custom-call | tf_op jit(solution)/shard_map/finish/pallas_call | solution.py:289
  (2 shorter events, 0.1 us)
Async XLA Ops:
  3.2 36.8 %all-to-all-start = ((bf16[32,56,128]{2,1,0:T(8,128)(2,1)}), bf16[32,56,128]{2,1,0:T(8,128)(2,1)S(1)}, u32[]{:S(2)}, u32[]{:S(2)}) async-start(bf16[32,56,128]{2,1,0:T(8,128)(2,1)} %get-tuple-element.15), calls=%async_computation | async-start | bytes 917504 | tf_op jit(solution)/shard_map/all_to_all | solution.py:332
  10.5 15.3 %collective-permute-start = (bf16[20,8,128]{2,1,0:T(8,128)(2,1)S(1)}, bf16[20,8,128]{2,1,0:T(8,128)(2,1)S(1)}, u32[]{:S(2)}, u32[]{:S(2)}) collective-permute-start(bf16[20,8,128]{2,1,0:T(8,128)(2,1)S(1)} %get-tuple-element.17), channel_id=1, source_target_pairs={{0,16},{8,24},{16,0},{24,8},{1,17},{9,25},{17,1},{25,9},{2,18},{10... | collective-permute-start | bytes 122888 | tf_op jit(solution)/shard_map/ppermute | solution.py:331
  25.8 1.3 %collective-permute-start.1 = (bf16[2,20,8,128]{3,2,1,0:T(8,128)(2,1)S(1)}, bf16[2,20,8,128]{3,2,1,0:T(8,128)(2,1)S(1)}, u32[]{:S(2)}, u32[]{:S(2)}) collective-permute-start(bf16[2,20,8,128]{3,2,1,0:T(8,128)(2,1)S(1)} %pad_maximum_fusion.mine_ref), channel_id=1, source_target_pairs={{0,1},{1,0},{2,3},{3,2},{4,5},{5,4},{6,7},{7,6},{8,9},{9,8},{10,11... | collective-permute-start | bytes 245768 | tf_op jit(solution)/shard_map/ppermute | solution.py:334
  27.2 6.5 %collective-permute-start.2 = (bf16[4,5,8,128]{3,2,1,0:T(8,128)(2,1)S(1)}, bf16[4,5,8,128]{3,2,1,0:T(8,128)(2,1)S(1)}, u32[]{:S(2)}, u32[]{:S(2)}) collective-permute-start(bf16[4,5,8,128]{3,2,1,0:T(8,128)(2,1)S(1)} %get-tuple-element.19), channel_id=1, source_target_pairs={{0,2},{1,3},{2,4},{3,5},{4,6},{5,7},{6,0},{7,1},{8,10},{9,11},{10,... | collective-permute-start | bytes 122888 | tf_op jit(solution)/shard_map/ppermute | solution.py:340
  28.8 5.0 %collective-permute-start.3 = (bf16[4,5,8,128]{3,2,1,0:T(8,128)(2,1)S(1)}, bf16[4,5,8,128]{3,2,1,0:T(8,128)(2,1)S(1)}, u32[]{:S(2)}, u32[]{:S(2)}) collective-permute-start(bf16[4,5,8,128]{3,2,1,0:T(8,128)(2,1)S(1)} %get-tuple-element.20), channel_id=1, source_target_pairs={{0,4},{1,5},{2,6},{3,7},{4,0},{5,1},{6,2},{7,3},{8,12},{9,13},{10,... | collective-permute-start | bytes 122888 | tf_op jit(solution)/shard_map/ppermute | solution.py:340
  30.3 7.3 %collective-permute-start.4 = (bf16[4,5,8,128]{3,2,1,0:T(8,128)(2,1)S(1)}, bf16[4,5,8,128]{3,2,1,0:T(8,128)(2,1)S(1)}, u32[]{:S(2)}, u32[]{:S(2)}) collective-permute-start(bf16[4,5,8,128]{3,2,1,0:T(8,128)(2,1)S(1)} %get-tuple-element.21), channel_id=1, source_target_pairs={{0,6},{1,7},{2,0},{3,1},{4,2},{5,3},{6,4},{7,5},{8,14},{9,15},{10,... | collective-permute-start | bytes 122888 | tf_op jit(solution)/shard_map/ppermute | solution.py:340
  31.7 5.8 %collective-permute-start.5 = (bf16[4,5,8,128]{3,2,1,0:T(8,128)(2,1)S(1)}, bf16[4,5,8,128]{3,2,1,0:T(8,128)(2,1)S(1)}, u32[]{:S(2)}, u32[]{:S(2)}) collective-permute-start(bf16[4,5,8,128]{3,2,1,0:T(8,128)(2,1)S(1)} %get-tuple-element.22), channel_id=1, source_target_pairs={{0,8},{1,9},{2,10},{3,11},{4,12},{5,13},{6,14},{7,15},{8,0},{9,1},... | collective-permute-start | bytes 122888 | tf_op jit(solution)/shard_map/ppermute | solution.py:340
  31.7 6.2 %collective-permute-start.6 = (bf16[4,5,8,128]{3,2,1,0:T(8,128)(2,1)S(1)}, bf16[4,5,8,128]{3,2,1,0:T(8,128)(2,1)S(1)}, u32[]{:S(2)}, u32[]{:S(2)}) collective-permute-start(bf16[4,5,8,128]{3,2,1,0:T(8,128)(2,1)S(1)} %get-tuple-element.23), channel_id=1, source_target_pairs={{0,10},{1,11},{2,12},{3,13},{4,14},{5,15},{6,8},{7,9},{8,2},{9,3},... | collective-permute-start | bytes 122888 | tf_op jit(solution)/shard_map/ppermute | solution.py:340
  33.7 4.9 %collective-permute-start.7 = (bf16[4,5,8,128]{3,2,1,0:T(8,128)(2,1)S(1)}, bf16[4,5,8,128]{3,2,1,0:T(8,128)(2,1)S(1)}, u32[]{:S(2)}, u32[]{:S(2)}) collective-permute-start(bf16[4,5,8,128]{3,2,1,0:T(8,128)(2,1)S(1)} %get-tuple-element.24), channel_id=1, source_target_pairs={{0,12},{1,13},{2,14},{3,15},{4,8},{5,9},{6,10},{7,11},{8,4},{9,5},... | collective-permute-start | bytes 122888 | tf_op jit(solution)/shard_map/ppermute | solution.py:340
  33.8 6.2 %collective-permute-start.8 = (bf16[4,5,8,128]{3,2,1,0:T(8,128)(2,1)S(1)}, bf16[4,5,8,128]{3,2,1,0:T(8,128)(2,1)S(1)}, u32[]{:S(2)}, u32[]{:S(2)}) collective-permute-start(bf16[4,5,8,128]{3,2,1,0:T(8,128)(2,1)S(1)} %get-tuple-element.25), channel_id=1, source_target_pairs={{0,14},{1,15},{2,8},{3,9},{4,10},{5,11},{6,12},{7,13},{8,6},{9,7},... | collective-permute-start | bytes 122888 | tf_op jit(solution)/shard_map/ppermute | solution.py:340
